TPU v7x, 128 devices: a whole 4x4x4 slice. The times are simulated.
128 devices in a mesh: data: 1, ctxo: 2 (over core), ctx: 64 (over z, y, x).
Axes of the slice: x: 4, y: 4, z: 4, core: 2. Of those that a mesh axis runs over, the one named last changes fastest.
Arguments:
- q_seq: bfloat16 [1, 24576, 4, 128], P('data', ('ctxo', 'ctx'))
- k_seq: bfloat16 [1, 24576, 1, 128], P('data', ('ctxo', 'ctx'))
- v_seq: bfloat16 [1, 24576, 1, 128], P('data', ('ctxo', 'ctx'))
- do_seq: bfloat16 [1, 24576, 4, 128], P('data', ('ctxo', 'ctx'))
Outputs:
- output 1: bfloat16 [1, 24576, 4, 128], P('data', ('ctxo', 'ctx'))
- output 2: bfloat16 [1, 24576, 4, 128], P('data', ('ctxo', 'ctx'))
- output 3: bfloat16 [1, 24576, 1, 128], P('data', ('ctxo', 'ctx'))
- output 4: bfloat16 [1, 24576, 1, 128], P('data', ('ctxo', 'ctx'))
All inputs are finite; a program needn't handle non-finite values.
Results may differ from a plain program's by a relative error of at most 0.0106846.
Values are sent between devices in bfloat16 or wider.
A program may use at most 1 GiB of HBM per device.

v0:
```python
import math
import jax
import jax.numpy as jnp
from jax import lax
from jax.sharding import PartitionSpec as P

CTX_AXES = ('ctxo', 'ctx')


def causal_mask(n_rows):
    row_ids = lax.broadcasted_iota(jnp.int32, (n_rows, 1, n_rows), 0)
    col_ids = lax.broadcasted_iota(jnp.int32, (n_rows, 1, n_rows), 2)
    return row_ids >= col_ids


def pair_forward(q_blk, k_blk, v_blk, key_mask):
    q_scale = 1.0 / math.sqrt(q_blk.shape[-1])
    scores = jnp.einsum('bqhgd,bkhd->bhqgk', q_blk, k_blk, preferred_element_type=jnp.float32) * q_scale
    if key_mask is not None:
        scores = jnp.where(key_mask, scores, -jnp.inf)
    row_max = jnp.max(scores, axis=-1)
    prob_blk = jnp.exp(scores - row_max[..., None])
    row_sum = jnp.sum(prob_blk, axis=-1)
    out_blk = jnp.einsum('bhqgk,bkhd->bhqgd', prob_blk.astype(jnp.bfloat16), v_blk, preferred_element_type=jnp.float32)
    return out_blk / row_sum[..., None], row_max + jnp.log(row_sum)


def merge_parts(out_a, lse_a, out_b, lse_b):
    lse_new = jnp.logaddexp(lse_a, lse_b)
    out_new = out_a * jnp.exp(lse_a - lse_new)[..., None] + out_b * jnp.exp(lse_b - lse_new)[..., None]
    return out_new, lse_new


def pair_backward(q_blk, do_blk, lse_blk, drow_blk, k_blk, v_blk, key_mask):
    q_scale = 1.0 / math.sqrt(q_blk.shape[-1])
    scores = jnp.einsum('bqhgd,bkhd->bhqgk', q_blk, k_blk, preferred_element_type=jnp.float32) * q_scale
    if key_mask is not None:
        scores = jnp.where(key_mask, scores, -jnp.inf)
    prob_blk = jnp.exp(scores - lse_blk[..., None])
    dv_part = jnp.einsum('bhqgk,bqhgd->bhkd', prob_blk.astype(jnp.bfloat16), do_blk, preferred_element_type=jnp.float32)
    prob_grad = jnp.einsum('bqhgd,bkhd->bhqgk', do_blk, v_blk, preferred_element_type=jnp.float32)
    score_grad = (prob_blk * (prob_grad - drow_blk[..., None])).astype(jnp.bfloat16)
    dq_part = jnp.einsum('bhqgk,bkhd->bhqgd', score_grad, k_blk, preferred_element_type=jnp.float32) * q_scale
    dk_part = jnp.einsum('bhqgk,bqhgd->bhkd', score_grad, q_blk, preferred_element_type=jnp.float32) * q_scale
    return dq_part, dk_part, dv_part


def solution(mesh):
    n_ctx = mesh.shape['ctxo'] * mesh.shape['ctx']
    half_ctx = n_ctx // 2
    next_perm = [(src_idx, (src_idx + 1) % n_ctx) for src_idx in range(n_ctx)]
    home_kv = [(src_idx, (src_idx - half_ctx) % n_ctx) for src_idx in range(n_ctx)]
    home_q = [(src_idx, (src_idx - half_ctx + 1) % n_ctx) for src_idx in range(n_ctx)]
    blk_spec = P('data', CTX_AXES, None, None)

    def send_next(tree_in):
        return lax.ppermute(tree_in, CTX_AXES, next_perm)

    def local_attn(q_in, k_in, v_in, do_in):
        batch_rows, chunk_len, q_heads, head_dim = q_in.shape
        kv_heads = k_in.shape[2]
        row_shape = (batch_rows, chunk_len, kv_heads, q_heads // kv_heads, head_dim)
        rank_idx = lax.axis_index(CTX_AXES)
        q_own = q_in.reshape(row_shape)
        do_own = do_in.reshape(row_shape)
        diag_mask = causal_mask(chunk_len)
        last_owner = rank_idx >= half_ctx

        own_out, own_lse = pair_forward(q_own, k_in, v_in, diag_mask)

        def fwd_step(step_idx, state_in):
            own_out, own_lse, k_buf, v_buf, q_buf, hlp_out, hlp_lse = state_in
            k_buf, v_buf, q_buf, hlp_out, hlp_lse = send_next((k_buf, v_buf, q_buf, hlp_out, hlp_lse))
            is_owner = rank_idx >= step_idx
            part_out, part_lse = pair_forward(jnp.where(is_owner, q_own, q_buf), jnp.where(is_owner, k_buf, k_in), jnp.where(is_owner, v_buf, v_in), None)
            new_out, new_lse = merge_parts(jnp.where(is_owner, own_out, hlp_out), jnp.where(is_owner, own_lse, hlp_lse), part_out, part_lse)
            own_out = jnp.where(is_owner, new_out, own_out)
            own_lse = jnp.where(is_owner, new_lse, own_lse)
            hlp_out = jnp.where(is_owner, hlp_out, new_out)
            hlp_lse = jnp.where(is_owner, hlp_lse, new_lse)
            return own_out, own_lse, k_buf, v_buf, q_buf, hlp_out, hlp_lse

        fwd_state = (own_out, own_lse, k_in, v_in, q_own, jnp.zeros_like(own_out), jnp.full_like(own_lse, -jnp.inf))
        own_out, own_lse, k_buf, v_buf, q_buf, hlp_out, hlp_lse = lax.fori_loop(1, half_ctx, fwd_step, fwd_state)
        k_buf, v_buf = send_next((k_buf, v_buf))
        part_out, part_lse = pair_forward(q_own, k_buf, v_buf, None)
        new_out, new_lse = merge_parts(own_out, own_lse, part_out, part_lse)
        own_out = jnp.where(last_owner, new_out, own_out)
        own_lse = jnp.where(last_owner, new_lse, own_lse)
        hlp_out, hlp_lse = lax.ppermute((hlp_out, hlp_lse), CTX_AXES, home_q)
        own_out, own_lse = merge_parts(own_out, own_lse, hlp_out, hlp_lse)

        drow_own = jnp.sum(jnp.swapaxes(do_own, 1, 2) * own_out, axis=-1)
        dq_own, dk_own, dv_own = pair_backward(q_own, do_own, own_lse, drow_own, k_in, v_in, diag_mask)

        def bwd_step(step_idx, state_in):
            dq_own, dk_own, dv_own, kv_bundle, q_bundle = state_in
            kv_bundle, q_bundle = send_next((kv_bundle, q_bundle))
            k_buf, v_buf, dk_buf, dv_buf = kv_bundle
            q_buf, do_buf, lse_buf, drow_buf, dq_buf = q_bundle
            is_owner = rank_idx >= step_idx
            dq_part, dk_part, dv_part = pair_backward(
                jnp.where(is_owner, q_own, q_buf), jnp.where(is_owner, do_own, do_buf),
                jnp.where(is_owner, own_lse, lse_buf), jnp.where(is_owner, drow_own, drow_buf),
                jnp.where(is_owner, k_buf, k_in), jnp.where(is_owner, v_buf, v_in), None)
            dq_own = jnp.where(is_owner, dq_own + dq_part, dq_own)
            dk_own = jnp.where(is_owner, dk_own, dk_own + dk_part)
            dv_own = jnp.where(is_owner, dv_own, dv_own + dv_part)
            kv_bundle = (k_buf, v_buf, jnp.where(is_owner, dk_buf + dk_part, dk_buf), jnp.where(is_owner, dv_buf + dv_part, dv_buf))
            q_bundle = (q_buf, do_buf, lse_buf, drow_buf, jnp.where(is_owner, dq_buf, dq_buf + dq_part))
            return dq_own, dk_own, dv_own, kv_bundle, q_bundle

        kv_bundle = (k_in, v_in, jnp.zeros_like(dk_own), jnp.zeros_like(dv_own))
        q_bundle = (q_own, do_own, own_lse, drow_own, jnp.zeros_like(dq_own))
        dq_own, dk_own, dv_own, kv_bundle, q_bundle = lax.fori_loop(1, half_ctx, bwd_step, (dq_own, dk_own, dv_own, kv_bundle, q_bundle))
        k_buf, v_buf, dk_buf, dv_buf = send_next(kv_bundle)
        dq_part, dk_part, dv_part = pair_backward(q_own, do_own, own_lse, drow_own, k_buf, v_buf, None)
        dq_own = jnp.where(last_owner, dq_own + dq_part, dq_own)
        dk_buf = jnp.where(last_owner, dk_buf + dk_part, dk_buf)
        dv_buf = jnp.where(last_owner, dv_buf + dv_part, dv_buf)
        dk_buf, dv_buf = lax.ppermute((dk_buf, dv_buf), CTX_AXES, home_kv)
        dq_buf = lax.ppermute(q_bundle[4], CTX_AXES, home_q)
        out_seq = jnp.swapaxes(own_out.astype(jnp.bfloat16), 1, 2).reshape(q_in.shape)
        dq_seq = jnp.swapaxes((dq_own + dq_buf).astype(jnp.bfloat16), 1, 2).reshape(q_in.shape)
        dk_seq = jnp.swapaxes((dk_own + dk_buf).astype(jnp.bfloat16), 1, 2)
        dv_seq = jnp.swapaxes((dv_own + dv_buf).astype(jnp.bfloat16), 1, 2)
        return out_seq, dq_seq, dk_seq, dv_seq

    return jax.shard_map(local_attn, mesh=mesh, in_specs=(blk_spec, blk_spec, blk_spec, blk_spec), out_specs=(blk_spec, blk_spec, blk_spec, blk_spec), check_vma=False)
```

profile of v0, /device:TPU:0, one launch (start us, length us, event | category | flops | bytes accessed | tf_op | source)
XLA Modules:
  0.0 3677.8 jit_solution(678242575029006939)
XLA Ops:
  4.5 1259.6 %while.62 = (s32[]{:T(128)}, f32[1,1,192,4,128]{4,2,3,1,0:T(8,128)S(1)}, f32[1,1,192,4]{2,3,1,0:T(4,128)S(1)}, bf16[1,192,1,128]{3,1,2,0:T(8,128)(2,1)S(1)}, bf1...) while((s32[]{:T(128)}, ...), condition=%wide.region_5.6_spmd.clone, body=%wide.region_2.5_spmd.clone.sunk | while | flops 77327616 | bytes 8144229 | solution.py:84
  31.3 14.5 collective-permute-done.2
  52.7 15.7 collective-permute-done.2
  75.3 15.2 collective-permute-done.2
  97.4 14.7 collective-permute-done.2
  119.0 14.2 collective-permute-done.2
  140.1 13.7 collective-permute-done.2
  160.7 13.2 collective-permute-done.2
  180.9 12.8 collective-permute-done.2
  200.5 12.8 collective-permute-done.2
  219.6 12.8 collective-permute-done.2
  238.2 12.8 collective-permute-done.2
  256.4 12.8 collective-permute-done.2
  274.0 12.8 collective-permute-done.2
  291.1 12.8 collective-permute-done.2
  308.2 12.8 collective-permute-done.2
  877.2 12.8 collective-permute-done.2
  896.9 12.8 collective-permute-done.2
  916.2 12.8 collective-permute-done.2
  935.0 12.8 collective-permute-done.2
  1225.3 12.5 collective-permute-done.2
  1244.7 13.0 collective-permute-done.2
  1273.6 13.6 collective-permute-done.16
  1290.8 2354.0 %while.63 = (s32[]{:T(128)}, f32[1,1,192,4,128]{4,2,3,1,0:T(8,128)S(1)}, f32[1,1,192,128]{3,2,1,0:T(8,128)S(1)}, f32[1,1,192,128]{3,2,1,0:T(8,128)S(1)}, bf16[1,...) while((s32[]{:T(128)}, ...), condition=%wide.region_10.11_spmd.clone, body=%wide.region_9.10_spmd.clone.sunk | while | flops 190957056 | bytes 13628005 | solution.py:115
  1291.4 16.5 collective-permute-done.6
  1333.3 15.1 collective-permute-done.6
  1373.3 14.6 collective-permute-done.6
  1413.4 14.0 collective-permute-done.6
  1452.9 12.9 collective-permute-done.6
  1490.8 12.3 collective-permute-done.6
  1528.0 12.3 collective-permute-done.6
  1565.1 12.3 collective-permute-done.6
  1602.3 12.3 collective-permute-done.6
  1639.4 12.3 collective-permute-done.6
  1676.6 12.3 collective-permute-done.6
  1713.7 12.3 collective-permute-done.6
  1750.9 12.3 collective-permute-done.6
  1788.0 12.3 collective-permute-done.6
  1825.2 12.3 collective-permute-done.6
  1862.3 12.3 collective-permute-done.6
  1899.5 12.3 collective-permute-done.6
  1936.6 12.3 collective-permute-done.6
  1973.8 12.3 collective-permute-done.6
  2010.9 12.3 collective-permute-done.6
  2048.0 12.3 collective-permute-done.6
  2085.2 12.3 collective-permute-done.6
  2122.3 12.3 collective-permute-done.6
  2159.5 12.3 collective-permute-done.6
  2196.6 12.3 collective-permute-done.6
  2233.8 12.3 collective-permute-done.6
  2270.9 12.3 collective-permute-done.6
  2308.1 12.3 collective-permute-done.6
  2345.2 12.3 collective-permute-done.6
  2382.4 12.3 collective-permute-done.6
  2419.5 12.3 collective-permute-done.6
  2456.7 12.3 collective-permute-done.6
  2493.8 12.3 collective-permute-done.6
  2531.0 12.3 collective-permute-done.6
  2568.1 12.3 collective-permute-done.6
  2605.2 12.3 collective-permute-done.6
  2642.4 12.3 collective-permute-done.6
  2679.5 12.3 collective-permute-done.6
  2716.7 12.3 collective-permute-done.6
  3654.1 16.0 collective-permute-done.19
  (3547 shorter events, 2858.8 us)
Async XLA Ops:
  1290.9 41.5 %collective-permute-start.5 = (f32[1,1,192,4,128]{4,2,3,1,0:T(8,128)S(1)}, f32[1,1,192,4,128]{4,2,3,1,0:T(8,128)S(1)}, u32[]{:S(2)}, u32[]{:S(2)}) collective-permute-start(f32[1,1,192,4,128]{4,2,3,1,0:T(8,128)S(1)} %broadcast_select_fusion.33), channel_id=1, source_target_pairs={{0,1},{1,2},{2,3},{3,4},{4,5},{5,6},{6,7},{7,8},{8,9},{9,10},{10,1... | collective-permute-start | bytes 1179656 | tf_op jit(solution)/shard_map/while/body/eval_jaxpr/ppermute | solution.py:57
  1291.0 32.0 collective-permute-start.7
  1332.8 39.6 %collective-permute-start.5 = (f32[1,1,192,4,128]{4,2,3,1,0:T(8,128)S(1)}, f32[1,1,192,4,128]{4,2,3,1,0:T(8,128)S(1)}, u32[]{:S(2)}, u32[]{:S(2)}) collective-permute-start(f32[1,1,192,4,128]{4,2,3,1,0:T(8,128)S(1)} %broadcast_select_fusion.33), channel_id=1, source_target_pairs={{0,1},{1,2},{2,3},{3,4},{4,5},{5,6},{6,7},{7,8},{8,9},{9,10},{10,1... | collective-permute-start | bytes 1179656 | tf_op jit(solution)/shard_map/while/body/eval_jaxpr/ppermute | solution.py:57
  1372.8 39.7 %collective-permute-start.5 = (f32[1,1,192,4,128]{4,2,3,1,0:T(8,128)S(1)}, f32[1,1,192,4,128]{4,2,3,1,0:T(8,128)S(1)}, u32[]{:S(2)}, u32[]{:S(2)}) collective-permute-start(f32[1,1,192,4,128]{4,2,3,1,0:T(8,128)S(1)} %broadcast_select_fusion.33), channel_id=1, source_target_pairs={{0,1},{1,2},{2,3},{3,4},{4,5},{5,6},{6,7},{7,8},{8,9},{9,10},{10,1... | collective-permute-start | bytes 1179656 | tf_op jit(solution)/shard_map/while/body/eval_jaxpr/ppermute | solution.py:57
  1412.9 39.0 %collective-permute-start.5 = (f32[1,1,192,4,128]{4,2,3,1,0:T(8,128)S(1)}, f32[1,1,192,4,128]{4,2,3,1,0:T(8,128)S(1)}, u32[]{:S(2)}, u32[]{:S(2)}) collective-permute-start(f32[1,1,192,4,128]{4,2,3,1,0:T(8,128)S(1)} %broadcast_select_fusion.33), channel_id=1, source_target_pairs={{0,1},{1,2},{2,3},{3,4},{4,5},{5,6},{6,7},{7,8},{8,9},{9,10},{10,1... | collective-permute-start | bytes 1179656 | tf_op jit(solution)/shard_map/while/body/eval_jaxpr/ppermute | solution.py:57
  1452.4 37.4 %collective-permute-start.5 = (f32[1,1,192,4,128]{4,2,3,1,0:T(8,128)S(1)}, f32[1,1,192,4,128]{4,2,3,1,0:T(8,128)S(1)}, u32[]{:S(2)}, u32[]{:S(2)}) collective-permute-start(f32[1,1,192,4,128]{4,2,3,1,0:T(8,128)S(1)} %broadcast_select_fusion.33), channel_id=1, source_target_pairs={{0,1},{1,2},{2,3},{3,4},{4,5},{5,6},{6,7},{7,8},{8,9},{9,10},{10,1... | collective-permute-start | bytes 1179656 | tf_op jit(solution)/shard_map/while/body/eval_jaxpr/ppermute | solution.py:57
  1490.3 36.7 collective-permute-start.5
  1527.5 36.7 collective-permute-start.5
  1564.7 36.7 collective-permute-start.5
  1601.8 36.7 collective-permute-start.5
  1638.9 36.7 collective-permute-start.5
  1676.1 36.7 collective-permute-start.5
  1713.2 36.7 collective-permute-start.5
  1750.4 36.7 collective-permute-start.5
  1787.5 36.7 collective-permute-start.5
  1824.7 36.7 collective-permute-start.5
  1861.8 36.7 collective-permute-start.5
  1899.0 36.7 collective-permute-start.5
  1936.1 36.7 collective-permute-start.5
  1973.3 36.7 collective-permute-start.5
  2010.4 36.7 collective-permute-start.5
  2047.5 36.7 collective-permute-start.5
  2084.7 36.7 collective-permute-start.5
  2121.8 36.7 collective-permute-start.5
  2159.0 36.7 collective-permute-start.5
  2196.1 36.7 collective-permute-start.5
  2233.3 36.7 collective-permute-start.5
  2270.4 36.7 collective-permute-start.5
  2307.6 36.7 collective-permute-start.5
  2344.7 36.7 collective-permute-start.5
  2381.9 36.7 collective-permute-start.5
  2419.0 36.7 collective-permute-start.5
  2456.2 36.7 collective-permute-start.5
  2493.3 36.7 collective-permute-start.5
  2530.5 36.7 collective-permute-start.5
  2567.6 36.7 collective-permute-start.5
  2604.8 36.7 collective-permute-start.5
  2641.9 36.7 collective-permute-start.5
  2679.1 36.7 collective-permute-start.5
  2716.2 36.7 collective-permute-start.5
  2753.3 36.7 collective-permute-start.5
  2790.5 36.7 collective-permute-start.5
  2827.6 36.7 collective-permute-start.5
  2864.8 36.7 collective-permute-start.5
  2901.9 36.7 collective-permute-start.5
  2939.1 36.7 collective-permute-start.5
  2976.2 36.7 collective-permute-start.5
  3013.4 36.7 collective-permute-start.5
  3050.5 36.7 collective-permute-start.5
  3087.7 36.7 collective-permute-start.5
  3124.8 36.7 collective-permute-start.5
  3161.9 36.7 collective-permute-start.5
  3199.1 36.7 collective-permute-start.5
  3236.2 36.7 collective-permute-start.5
  3273.4 36.7 collective-permute-start.5
  3310.5 36.7 collective-permute-start.5
  3347.7 36.7 collective-permute-start.5
  3384.8 36.7 collective-permute-start.5
  3422.0 36.7 collective-permute-start.5
  3459.1 36.7 collective-permute-start.5
  3496.3 36.7 collective-permute-start.5
  3533.4 36.7 collective-permute-start.5
  3570.6 36.7 collective-permute-start.5
  3607.7 36.7 collective-permute-start.5
  (902 other events, 13531.5 us)
where the time goes:
time: 3680 us
  waiting for transfers between devices  2930 us (80%)
  starting transfers between devices  421 us (11%)
  matrix products  160 us (4%)
  local copies, waits for them, and re-layouts  132 us (4%)
    ppermute x888, waiting for transfers between devices, send_next(): return lax.ppermute(tree_in, CTX_AXES, next_perm)  2910 us
    ppermute x888, starting transfers between devices, send_next(): return lax.ppermute(tree_in, CTX_AXES, next_perm)  420 us
    while x693, local copies, waits for them, and re-layouts  124 us
  transfers between devices with their start and end apart: 893, of which 400 were waited for; matrix products, arithmetic and copies ran while one was open for 6% of the time, Pallas kernels for 0%

commit v1 on v0

v1 whole, which is shorter than its diff:
```python
import functools
import math
import jax
import jax.numpy as jnp
from jax import lax
from jax.experimental import pallas as pl
from jax.experimental.pallas import tpu as pltpu
from jax.sharding import PartitionSpec as P

CTX_AXES = ('ctxo', 'ctx')
MESH = pl.DeviceIdType.MESH
f32 = jnp.float32
bf16 = jnp.bfloat16
i32 = jnp.int32

ROWS = 768
HD = 128
SUB = 48
T = 256
NT = ROWS // T
SCALE = 1.0 / math.sqrt(HD)
SCALE2 = SCALE * math.log2(math.e)
NEG = -1e30
QUAD = 4
TRIO = 3
OFFS = (1, 2, 3)
TILES = range(NT)
N_FULL = 14


def dot(a, b, ca, cb):
    return lax.dot_general(a, b, (((ca,), (cb,)), ((), ())), preferred_element_type=f32)


def tile(n):
    return slice(n * T, (n + 1) * T)


def body(q_in, k_in, v_in, do_in, o_out, dq_out, dk_out, dv_out,
         q_all, do_all, k_all, v_all, kt, vt, ot, dqt, dk, dv, cache, tb, dpb,
         m_run, l_run, lse, dd, stat_all,
         or1, or2, dqr1, dqr2, dkr1, dvr1, dk2, dv2, dkr2, dvr2, kst, vst, dk_fin, dv_fin,
         ka_ss, ka_rs, va_ss, va_rs, kx_ss, kx_rs, ky_ss, ky_rs, vy_ss, vy_rs, vx_ss, vx_rs,
         q_ss, q_rs, do_ss, do_rs, st_ss, st_rs, o1_ss, o1_rs, o2_ss, o2_rs,
         g1_ss, g1_rs, g2_ss, g2_rs, rk1_ss, rk1_rs, rv1_ss, rv1_rs, rk2_ss, rk2_rs, rv2_ss, rv2_rs,
         fk_ss, fk_rs, fv_ss, fv_rs):
    a = lax.axis_index('ctxo')
    b = lax.axis_index('ctx')
    z = b // 16
    y = (b // 4) % 4
    x = b % 4
    m_blk = 4 * y + x
    i_own = 4 * a + z
    pa = 1 - a
    par = (a + z) % 2

    def dev(a_, z_, y_, x_):
        return {'ctxo': a_, 'ctx': 16 * z_ + 4 * y_ + x_}

    def rc(src, dst, ss, rs, to):
        return pltpu.make_async_remote_copy(src_ref=src, dst_ref=dst, send_sem=ss, recv_sem=rs, device_id=to, device_id_type=MESH)

    partner = dev(pa, z, y, x)

    def got(ref, ss, rs):
        rc(ref, ref, ss, rs, partner).wait_recv()

    def sent(ref, ss, rs):
        rc(ref, ref, ss, rs, partner).wait_send()

    def zpeer(d):
        return (z + d) % 4

    def group_of(s):
        a_s = s // 2
        return a_s, 2 * (s % 2) + (a_s + a) % 2

    bar = pltpu.get_barrier_semaphore()
    for d in OFFS:
        pl.semaphore_signal(bar, inc=1, device_id=dev(a, zpeer(d), y, x), device_id_type=MESH)
        pl.semaphore_signal(bar, inc=1, device_id=dev(pa, zpeer(d), y, x), device_id_type=MESH)
        pl.semaphore_signal(bar, inc=1, device_id=dev(a, z, (y + d) % 4, x), device_id_type=MESH)
        pl.semaphore_signal(bar, inc=1, device_id=dev(a, z, y, (x + d) % 4), device_id_type=MESH)
    pl.semaphore_signal(bar, inc=1, device_id=partner, device_id_type=MESH)
    pl.semaphore_wait(bar, 13)

    k5 = k_all.reshape(4, 4, 4, SUB, HD)
    v5 = v_all.reshape(4, 4, 4, SUB, HD)

    s_me = 2 * a + z // 2
    keep = par == a
    for d in range(QUAD):
        zt = zpeer(d)
        rows = pl.ds(pl.multiple_of(SUB * zt, SUB), SUB)
        kc = rc(k_in.at[rows], k5.at[s_me, y, x], ka_ss.at[d], ka_rs.at[s_me], dev(par, zt, y, x))
        vc = rc(v_in.at[rows], v5.at[s_me, y, x], va_ss.at[d], va_rs.at[s_me], dev(par, zt, y, x))
        if d == 0:
            @pl.when(keep)
            def _():
                dst = pl.ds(pl.multiple_of(SUB * m_blk, SUB), SUB)
                k_all[s_me, dst, :] = k_in[rows, :]
                v_all[s_me, dst, :] = v_in[rows, :]

            @pl.when(jnp.logical_not(keep))
            def _():
                kc.start()
                vc.start()
        else:
            kc.start()
            vc.start()

    for d in OFFS:
        rc(q_in, q_all.at[i_own], q_ss.at[d], q_rs.at[i_own], dev(a, zpeer(d), y, x)).start()
    rc(q_in, q_all.at[i_own], q_ss.at[0], q_rs.at[i_own], partner).start()
    q_all[i_own] = q_in[...]
    do_all[i_own] = do_in[...]

    def wait_slot(s):
        a_s, z_s = group_of(s)
        mine = (a_s == a) & (z_s == z)

        @pl.when(jnp.logical_not(mine))
        def _():
            got(k5.at[s, y, x], ka_ss.at[0], ka_rs.at[s])
            got(v5.at[s, y, x], va_ss.at[0], va_rs.at[s])

    for s in range(QUAD):
        wait_slot(s)
    for d in OFFS:
        xt = dev(a, z, y, (x + d) % 4)
        yt = dev(a, z, (y + d) % 4, x)
        rc(k5.at[:, y, x], k5.at[:, y, x], kx_ss.at[d - 1], kx_rs.at[d - 1], xt).start()
        rc(v5.at[:, y, x], v5.at[:, y, x], vy_ss.at[d - 1], vy_rs.at[d - 1], yt).start()
    for d in OFFS:
        got(k5.at[:, y, (x - d) % 4], kx_ss.at[d - 1], kx_rs.at[d - 1])
        got(v5.at[:, (y - d) % 4, x], vy_ss.at[d - 1], vy_rs.at[d - 1])
    for d in OFFS:
        xt = dev(a, z, y, (x + d) % 4)
        yt = dev(a, z, (y + d) % 4, x)
        rc(k5.at[:, y], k5.at[:, y], ky_ss.at[d - 1], ky_rs.at[d - 1], yt).start()
        rc(v5.at[:, :, x], v5.at[:, :, x], vx_ss.at[d - 1], vx_rs.at[d - 1], xt).start()
    for d in OFFS:
        rc(do_in, do_all.at[i_own], do_ss.at[d], do_rs.at[i_own], dev(a, zpeer(d), y, x)).start()
    rc(do_in, do_all.at[i_own], do_ss.at[0], do_rs.at[i_own], partner).start()
    for d in OFFS:
        i_r = 4 * a + (z - d) % 4
        got(q_all.at[i_r], q_ss.at[0], q_rs.at[i_r])
        rc(q_all.at[i_r], q_all.at[i_r], q_ss.at[3 + d], q_rs.at[i_r], partner).start()

    dk[...] = jnp.zeros(dk.shape, f32)
    dv[...] = jnp.zeros(dv.shape, f32)
    dqt[...] = jnp.zeros(dqt.shape, f32)
    ot[...] = jnp.zeros(ot.shape, f32)
    m_run[...] = jnp.full(m_run.shape, NEG, f32)
    l_run[...] = jnp.zeros(l_run.shape, f32)

    for d in OFFS:
        got(k5.at[:, (y - d) % 4], ky_ss.at[d - 1], ky_rs.at[d - 1])
        got(v5.at[:, :, (x - d) % 4], vx_ss.at[d - 1], vx_rs.at[d - 1])
    for d in range(QUAD):
        i_r = 4 * pa + (z - d) % 4
        got(q_all.at[i_r], q_ss.at[0], q_rs.at[i_r])

    def transpose_kv(s, c):
        kt[s] = k_all[s].T
        vt[s] = v_all[s].T
        return c
    lax.fori_loop(0, 4, transpose_kv, 0)

    def full_count(i):
        n = jnp.int32(0)
        for s in range(QUAD):
            a_s, z_s = group_of(s)
            n = n + (4 * a_s + z_s < i).astype(i32)
        return n

    def cache_base(i):
        n = jnp.int32(0)
        for s in range(QUAD):
            a_s, z_s = group_of(s)
            n = n + jnp.maximum(i - 1 - 4 * a_s - z_s, 0)
        return n

    n_chunk = (SUB * (m_blk + 1) + T - 1) // T

    def seen(ch, ct):
        key_id = ch * T + lax.broadcasted_iota(i32, (T, T), 0)
        pos = (ct * T + lax.broadcasted_iota(i32, (1, T), 1)) // 4
        last = SUB * m_blk + jnp.clip(pos - SUB * z, -1, SUB - 1)
        return key_id <= last

    def rsum(p):
        return jnp.sum(p.reshape(p.shape[0] // 8, 8, p.shape[1]), axis=0)

    def rmax(p):
        return jnp.max(p.reshape(p.shape[0] // 8, 8, p.shape[1]), axis=0)

    def fwd_diag(i, s):
        def chunk(ch, c):
            rows = pl.ds(pl.multiple_of(ch * T, T), T)
            for ct in TILES:
                cs = tile(ct)
                t = dot(k_all[s, rows, :], q_all[i, cs, :], 1, 1) * SCALE2
                t = jnp.where(seen(ch, ct), t, -jnp.inf)
                m_old = m_run[i, :, cs]
                m_new = jnp.maximum(m_old, jnp.max(rmax(t), axis=0, keepdims=True))
                al = jnp.exp2(m_old - m_new)
                p = jnp.exp2(t - m_new)
                l_run[i, :, cs] = l_run[i, :, cs] * al + jnp.sum(rsum(p), axis=0, keepdims=True)
                ot[i, :, cs] = ot[i, :, cs] * al + dot(vt[s, :, rows], p.astype(bf16), 1, 0)
                m_run[i, :, cs] = m_new
            return c
        lax.fori_loop(0, n_chunk, chunk, 0)

    def fwd_scores(i, s, pc, ct, j, mx):
        t = dot(k_all[s, tile(j), :], q_all[i, tile(ct), :], 1, 1) * SCALE2
        cache[pc, tile(j), tile(ct)] = t
        r = rmax(t)
        return r if mx is None else jnp.maximum(mx, r)

    def fwd_full(i, n_i, base):
        @pl.when(n_i > 0)
        def _():
            mx = None
            for j in TILES:
                mx = fwd_scores(i, 0, base, 0, j, mx)

            def pair(s, mx):
                for ct in TILES:
                    cs = tile(ct)
                    s_n = s if ct < NT - 1 else jnp.minimum(s + 1, n_i - 1)
                    ct_n = (ct + 1) % NT
                    m_old = m_run[i, :, cs]
                    m_new = jnp.maximum(m_old, jnp.max(mx, axis=0, keepdims=True))
                    al = jnp.exp2(m_old - m_new)
                    mx2 = None
                    lp = None
                    o = None
                    for j in TILES:
                        mx2 = fwd_scores(i, s_n, base + s_n, ct_n, j, mx2)
                        p = jnp.exp2(cache[base + s, tile(j), cs] - m_new)
                        r = rsum(p)
                        lp = r if lp is None else lp + r
                        oj = dot(vt[s, :, tile(j)], p.astype(bf16), 1, 0)
                        o = oj if o is None else o + oj
                    l_run[i, :, cs] = l_run[i, :, cs] * al + jnp.sum(lp, axis=0, keepdims=True)
                    ot[i, :, cs] = ot[i, :, cs] * al + o
                    m_run[i, :, cs] = m_new
                    mx = mx2
                return mx
            lax.fori_loop(0, n_i, pair, mx)

    def stat_peer(off, sign):
        da, dz = divmod(off, 4)
        return (a + da) % 2, (z + sign * dz) % 4

    def fwd_step(n, c):
        i = 7 - n
        a_i = i // 4
        z_i = i % 4
        diag = (a_i + z_i) % 2 == a

        @pl.when(diag)
        def _():
            fwd_diag(i, 2 * a_i + z_i // 2)
        fwd_full(i, full_count(i), cache_base(i))

        @pl.when(n == 0)
        def _():
            for d in OFFS:
                i_r = 4 * a + (z - d) % 4
                got(do_all.at[i_r], do_ss.at[0], do_rs.at[i_r])
                rc(do_all.at[i_r], do_all.at[i_r], do_ss.at[3 + d], do_rs.at[i_r], partner).start()

        @pl.when(a_i != a)
        def _():
            got(do_all.at[i], do_ss.at[0], do_rs.at[i])
            rc(ot.at[i], or1.at[z_i], o1_ss.at[z_i], o1_rs.at[z_i], partner).start()
        d_part = jnp.sum(do_all[i].T.astype(f32) * ot[i], axis=0, keepdims=True)
        stat_all[i, i_own, 0:1, :] = m_run[i]
        stat_all[i, i_own, 1:2, :] = l_run[i]
        stat_all[i, i_own, 2:3, :] = d_part
        for off in range(1, 8):
            at, zt = stat_peer(off, 1)
            rc(stat_all.at[i, i_own], stat_all.at[i, i_own], st_ss.at[i, off - 1], st_rs.at[i, off - 1], dev(at, zt, y, x)).start()
        return c
    lax.fori_loop(0, 8, fwd_step, 0)

    def row_max(i):
        big = stat_all[i, 0, 0:1, :]
        for k in range(1, 8):
            big = jnp.maximum(big, stat_all[i, k, 0:1, :])
        return big

    def stats(i):
        for off in range(1, 8):
            af, zf = stat_peer(off, -1)
            got(stat_all.at[i, 4 * af + zf], st_ss.at[i, off - 1], st_rs.at[i, off - 1])
        big = row_max(i)
        tot = jnp.zeros((1, ROWS), f32)
        dsum = jnp.zeros((1, ROWS), f32)
        for k in range(8):
            w = jnp.exp2(stat_all[i, k, 0:1, :] - big)
            tot = tot + w * stat_all[i, k, 1:2, :]
            dsum = dsum + w * stat_all[i, k, 2:3, :]
        lse[i] = big + jnp.log(tot) * math.log2(math.e)
        dd[i] = dsum / tot

    def out_join(z_o):
        i = 4 * a + z_o
        got(or1.at[z_o], o1_ss.at[z_o], o1_rs.at[z_o])
        w_own = jnp.exp2(stat_all[i, i_own, 0:1, :] - lse[i])
        w_par = jnp.exp2(stat_all[i, 4 * pa + z, 0:1, :] - lse[i])
        for ct in TILES:
            cs = tile(ct)
            ot[i, :, cs] = ot[i, :, cs] * w_own[:, cs] + or1[z_o, :, cs] * w_par[:, cs]

        @pl.when(z_o != z)
        def _():
            h = (z_o - z) % 4 - 1
            rc(ot.at[i], or2.at[h], o2_ss.at[z_o], o2_rs.at[h], dev(a, z_o, y, x)).start()

    def dq_join(z_o):
        i = 4 * a + z_o
        got(dqr1.at[z_o], g1_ss.at[z_o], g1_rs.at[z_o])
        for ct in TILES:
            cs = tile(ct)
            dqt[i, :, cs] = dqt[i, :, cs] + dqr1[z_o, :, cs]

        @pl.when(z_o != z)
        def _():
            h = (z_o - z) % 4 - 1
            rc(dqt.at[i], dqr2.at[h], g2_ss.at[z_o], g2_rs.at[h], dev(a, z_o, y, x)).start()

    def grad_tile(i, s, t, rs, ct, slot):
        cs = tile(ct)
        p = jnp.exp2(t - lse[i, :, cs])
        ds = p * (dpb[slot] - dd[i, :, cs])
        return p.astype(bf16), ds.astype(bf16)

    def bwd_diag(i, s):
        def chunk(ch, c):
            rows = pl.ds(pl.multiple_of(ch * T, T), T)
            dv_c = None
            dk_c = None
            for ct in TILES:
                cs = tile(ct)
                t = dot(k_all[s, rows, :], q_all[i, cs, :], 1, 1) * SCALE2
                t = jnp.where(seen(ch, ct), t, -jnp.inf)
                dpb[ct] = dot(v_all[s, rows, :], do_all[i, cs, :], 1, 1)
                p, ds = grad_tile(i, s, t, rows, ct, ct)
                e = dot(p, do_all[i, cs, :], 1, 0)
                g = dot(ds, q_all[i, cs, :], 1, 0)
                dv_c = e if dv_c is None else dv_c + e
                dk_c = g if dk_c is None else dk_c + g
                dqt[i, :, cs] += dot(kt[s, :, rows], ds, 1, 0)
            dv[s, rows, :] += dv_c
            dk[s, rows, :] += dk_c
            return c
        lax.fori_loop(0, n_chunk, chunk, 0)

    def bwd_full(i, n_i, base):
        def d_scores(s, u):
            j, ct = divmod(u, NT)
            dpb[u % 3] = dot(v_all[s, tile(j), :], do_all[i, tile(ct), :], 1, 1)

        @pl.when(n_i > 0)
        def _():
            d_scores(0, 0)

            def pair(s, c):
                acc_v = None
                acc_k = None
                pend = None

                def products(u, p, ds, acc_v, acc_k):
                    j, ct = divmod(u, NT)
                    e = dot(p, do_all[i, tile(ct), :], 1, 0)
                    g = dot(ds, q_all[i, tile(ct), :], 1, 0)
                    acc_v = e if ct == 0 else acc_v + e
                    acc_k = g if ct == 0 else acc_k + g
                    dqt[i, :, tile(ct)] += dot(kt[s, :, tile(j)], ds, 1, 0)
                    if ct == NT - 1:
                        dv[s, tile(j), :] += acc_v
                        dk[s, tile(j), :] += acc_k
                    return acc_v, acc_k

                for u in range(NT * NT):
                    j, ct = divmod(u, NT)
                    if u < NT * NT - 1:
                        d_scores(s, u + 1)
                    else:
                        d_scores(jnp.minimum(s + 1, n_i - 1), 0)
                    now = grad_tile(i, s, cache[base + s, tile(j), tile(ct)], None, ct, u % 3)
                    if pend is not None:
                        acc_v, acc_k = products(u - 1, *pend, acc_v, acc_k)
                    pend = now
                products(NT * NT - 1, *pend, acc_v, acc_k)
                return c
            lax.fori_loop(0, n_i, pair, 0)

    dk5 = dk.reshape(4, 4, 4, SUB, HD)
    dv5 = dv.reshape(4, 4, 4, SUB, HD)
    dkr14 = dkr1.reshape(4, 3, 4, SUB, HD)
    dvr14 = dvr1.reshape(4, 3, 4, SUB, HD)
    dk24 = dk2.reshape(4, 4, SUB, HD)
    dv24 = dv2.reshape(4, 4, SUB, HD)

    def kv_first(s):
        for d in OFFS:
            yt = (y + d) % 4
            xt = (x + d) % 4
            rc(dk5.at[s, yt], dkr14.at[s, d - 1], rk1_ss.at[s, d - 1], rk1_rs.at[s, d - 1], dev(a, z, yt, x)).start()
            rc(dv5.at[s, :, xt], dvr14.at[s, d - 1], rv1_ss.at[s, d - 1], rv1_rs.at[s, d - 1], dev(a, z, y, xt)).start()

    def sub_rows(n):
        return pl.ds(pl.multiple_of(SUB * n, SUB), SUB)

    def kv_second(s):
        for d in OFFS:
            got(dkr14.at[s, d - 1], rk1_ss.at[s, d - 1], rk1_rs.at[s, d - 1])
            got(dvr14.at[s, d - 1], rv1_ss.at[s, d - 1], rv1_rs.at[s, d - 1])
        tot = dk[s, pl.ds(pl.multiple_of(4 * SUB * y, 4 * SUB), 4 * SUB), :]
        for d in range(TRIO):
            tot = tot + dkr1[s, d]
        dk2[s] = tot
        for n in range(QUAD):
            tot = dv[s, sub_rows(4 * n + x), :]
            for d in range(TRIO):
                tot = tot + dvr1[s, d, n * SUB:(n + 1) * SUB, :]
            dv2[s, n * SUB:(n + 1) * SUB, :] = tot
        for d in OFFS:
            yt = (y + d) % 4
            xt = (x + d) % 4
            rc(dk24.at[s, xt], dkr2.at[s, d - 1], rk2_ss.at[s, d - 1], rk2_rs.at[s, d - 1], dev(a, z, y, xt)).start()
            rc(dv24.at[s, yt], dvr2.at[s, d - 1], rv2_ss.at[s, d - 1], rv2_rs.at[s, d - 1], dev(a, z, yt, x)).start()

    def kv_third(s):
        for d in OFFS:
            got(dkr2.at[s, d - 1], rk2_ss.at[s, d - 1], rk2_rs.at[s, d - 1])
            got(dvr2.at[s, d - 1], rv2_ss.at[s, d - 1], rv2_rs.at[s, d - 1])
        tk = dk2[s, sub_rows(x), :]
        tv = dv2[s, sub_rows(y), :]
        for d in range(TRIO):
            tk = tk + dkr2[s, d]
            tv = tv + dvr2[s, d]
        kst[s] = (tk * SCALE).astype(bf16)
        vst[s] = tv.astype(bf16)
        a_s, z_s = group_of(s)
        mine = (a_s == a) & (z_s == z)
        h = (z_s - z) % 4
        rows = sub_rows(z)

        @pl.when(mine)
        def _():
            dk_fin[rows, :] = kst[s]
            dv_fin[rows, :] = vst[s]

        @pl.when(jnp.logical_not(mine))
        def _():
            rc(kst.at[s], dk_fin.at[rows], fk_ss.at[s], fk_rs.at[h], dev(a_s, z_s, y, x)).start()
            rc(vst.at[s], dv_fin.at[rows], fv_ss.at[s], fv_rs.at[h], dev(a_s, z_s, y, x)).start()

    def on_slot(i, fn):
        a_i = i // 4
        z_i = i % 4

        @pl.when((i >= 0) & (i < 8) & ((a_i + z_i) % 2 == a))
        def _():
            fn(2 * a_i + z_i // 2)

    def bwd_step(n, c):
        i = 7 - n
        a_i = i // 4
        z_i = i % 4

        @pl.when(n < 4)
        def _():
            stats(i)
            stats(i - 4)
            out_join(3 - n)

        @pl.when(n < 8)
        def _():
            bwd_full(i, full_count(i), cache_base(i))
        on_slot(i, lambda s: bwd_diag(i, s))
        on_slot(i, kv_first)

        @pl.when((n < 8) & (a_i != a))
        def _():
            rc(dqt.at[i], dqr1.at[z_i], g1_ss.at[z_i], g1_rs.at[z_i], partner).start()
        on_slot(i + 1, kv_second)
        on_slot(i + 2, kv_third)
        i1 = i + 1

        @pl.when((n >= 1) & (n <= 8) & (i1 // 4 == a))
        def _():
            dq_join(i1 % 4)
        return c
    lax.fori_loop(0, 10, bwd_step, 0)

    for h in range(TRIO):
        got(or2.at[h], o2_ss.at[0], o2_rs.at[h])
    for ct in TILES:
        cs = tile(ct)
        o_out[cs, :] = (ot[i_own, :, cs] + or2[0, :, cs] + or2[1, :, cs] + or2[2, :, cs]).T.astype(bf16)
    for h in range(TRIO):
        got(dqr2.at[h], g2_ss.at[0], g2_rs.at[h])
    for ct in TILES:
        cs = tile(ct)
        dq_out[cs, :] = ((dqt[i_own, :, cs] + dqr2[0, :, cs] + dqr2[1, :, cs] + dqr2[2, :, cs]).T * SCALE).astype(bf16)
    for h in range(QUAD):
        rows = sub_rows((z - h) % 4)

        def take():
            got(dk_fin.at[rows], fk_ss.at[0], fk_rs.at[h])
            got(dv_fin.at[rows], fv_ss.at[0], fv_rs.at[h])
        if h == 0:
            pl.when(jnp.logical_not(keep))(take)
        else:
            take()
    dk_out[...] = dk_fin[...]
    dv_out[...] = dv_fin[...]

    rows0 = pl.ds(0, SUB)
    for d in range(QUAD):
        def left():
            sent(k_in.at[rows0], ka_ss.at[d], ka_rs.at[0])
            sent(v_in.at[rows0], va_ss.at[d], va_rs.at[0])
        if d == 0:
            pl.when(jnp.logical_not(keep))(left)
        else:
            left()
    for d in range(TRIO):
        sent(k5.at[:, y, x], kx_ss.at[d], kx_rs.at[d])
        sent(v5.at[:, y, x], vy_ss.at[d], vy_rs.at[d])
        sent(k5.at[:, y], ky_ss.at[d], ky_rs.at[d])
        sent(v5.at[:, :, x], vx_ss.at[d], vx_rs.at[d])
    for d in range(7):
        sent(q_in, q_ss.at[d], q_rs.at[0])
        sent(do_in, do_ss.at[d], do_rs.at[0])

    def drain_i(i, c):
        for off in range(7):
            sent(stat_all.at[i, i_own], st_ss.at[i, off], st_rs.at[i, off])
        return c
    lax.fori_loop(0, 8, drain_i, 0)
    for n in range(QUAD):
        sent(ot.at[n], o1_ss.at[n], o1_rs.at[n])
        sent(ot.at[n], g1_ss.at[n], g1_rs.at[n])

        @pl.when(n != z)
        def _():
            sent(ot.at[n], o2_ss.at[n], o2_rs.at[0])
            sent(ot.at[n], g2_ss.at[n], g2_rs.at[0])
        for d in range(TRIO):
            sent(dkr14.at[0, 0], rk1_ss.at[n, d], rk1_rs.at[n, d])
            sent(dvr14.at[0, 0], rv1_ss.at[n, d], rv1_rs.at[n, d])
            sent(dkr2.at[0, 0], rk2_ss.at[n, d], rk2_rs.at[n, d])
            sent(dvr2.at[0, 0], rv2_ss.at[n, d], rv2_rs.at[n, d])
        a_s, z_s = group_of(n)

        @pl.when(jnp.logical_not((a_s == a) & (z_s == z)))
        def _():
            sent(kst.at[n], fk_ss.at[n], fk_rs.at[0])
            sent(vst.at[n], fv_ss.at[n], fv_rs.at[0])


def solution(mesh):
    blk_spec = P('data', CTX_AXES, None, None)

    def v(shape, dtype):
        return pltpu.VMEM(shape, dtype)

    def sem(*shape):
        return pltpu.SemaphoreType.DMA(shape)

    big = (ROWS, HD)
    scratch = [
        v((8,) + big, bf16), v((8,) + big, bf16),
        v((4,) + big, bf16), v((4,) + big, bf16),
        v((4, HD, ROWS), bf16), v((4, HD, ROWS), bf16),
        v((8, HD, ROWS), f32), v((8, HD, ROWS), f32),
        v((4,) + big, f32), v((4,) + big, f32),
        v((N_FULL, ROWS, ROWS), f32),
        v((1, 8, 128), f32), v((3, T, T), f32),
        v((8, 1, ROWS), f32), v((8, 1, ROWS), f32), v((8, 1, ROWS), f32), v((8, 1, ROWS), f32),
        v((8, 8, 3, ROWS), f32),
        v((4, HD, ROWS), f32), v((3, HD, ROWS), f32), v((4, HD, ROWS), f32), v((3, HD, ROWS), f32),
        v((4, 3, 4 * SUB, HD), f32), v((4, 3, 4 * SUB, HD), f32),
        v((4, 4 * SUB, HD), f32), v((4, 4 * SUB, HD), f32),
        v((4, 3, SUB, HD), f32), v((4, 3, SUB, HD), f32),
        v((4, SUB, HD), bf16), v((4, SUB, HD), bf16),
        v((4 * SUB, HD), bf16), v((4 * SUB, HD), bf16),
        *[sem(QUAD)] * 4, *[sem(TRIO)] * 8,
        *[sem(7), sem(8)] * 2, *[sem(8, 7)] * 2,
        *[sem(QUAD), sem(QUAD), sem(QUAD), sem(TRIO)] * 2,
        *[sem(QUAD, TRIO)] * 8, *[sem(QUAD)] * 4,
    ]
    call = pl.pallas_call(
        body,
        name='attn',
        out_shape=[jax.ShapeDtypeStruct(big, bf16), jax.ShapeDtypeStruct(big, bf16),
                   jax.ShapeDtypeStruct((4 * SUB, HD), bf16), jax.ShapeDtypeStruct((4 * SUB, HD), bf16)],
        in_specs=[pl.BlockSpec(memory_space=pltpu.VMEM)] * 4,
        out_specs=[pl.BlockSpec(memory_space=pltpu.VMEM)] * 4,
        scratch_shapes=scratch,
        compiler_params=pltpu.CompilerParams(collective_id=0, has_side_effects=True, vmem_limit_bytes=67043328),
    )

    def local_attn(q_in, k_in, v_in, do_in):
        o, dq, dk, dv = call(q_in.reshape(big), k_in.reshape(4 * SUB, HD), v_in.reshape(4 * SUB, HD), do_in.reshape(big))
        return o.reshape(q_in.shape), dq.reshape(q_in.shape), dk.reshape(k_in.shape), dv.reshape(k_in.shape)

    return jax.shard_map(local_attn, mesh=mesh, in_specs=(blk_spec,) * 4, out_specs=(blk_spec,) * 4, check_vma=False)
```

time: 3680 us -> 123 us (0.03)
  waiting for transfers between devices: 2930 us -> 0 us
  starting transfers between devices: 421 us -> 0 us
  matrix products: 160 us -> 0 us
  local copies, waits for them, and re-layouts: 132 us -> 3.95 us
  Pallas kernels: 0 us -> 118 us
    ppermute x893 -> x0, waiting for transfers between devices: 2930 us -> none  [the longest x888 2910 us: send_next(): return lax.ppermute(tree_in, CTX_AXES, next_perm)]
    ppermute x893 -> x0, starting transfers between devices: 421 us -> none  [the longest x888 420 us: send_next(): return lax.ppermute(tree_in, CTX_AXES, next_perm)]
    dot_general x454 -> x0, matrix products: 160 us -> none  [the longest x65 38.1 us: pair_forward(): jnp.einsum('bhqgk,bkhd->bhqgd', prob_blk.astype(jnp.bfloat16), v_blk, pre...]
    while x693 -> x0, local copies, waits for them, and re-layouts: 124 us -> none
    pallas_call x0 -> x1, Pallas kernels: none -> 118 us  [local_attn(): call(q_in.reshape(big), k_in.reshape(4 * SUB, HD), v_in.reshape(4 * SUB,...]
  transfers between devices with their start and end apart: 893 -> 0, of which waited for: 400 -> 0; matrix products, arithmetic and copies ran while one was open for 6% -> 0% of each run, Pallas kernels for 0% -> 0%
where the time goes in v1:
time: 123 us
  Pallas kernels  118 us (96%)
  local copies, waits for them, and re-layouts  3.95 us (3%)
    pallas_call x1, Pallas kernels, local_attn(): call(q_in.reshape(big), k_in.reshape(4 * SUB, HD), v_in.reshape(4 * SUB,...  118 us
    unnamed x10, local copies, waits for them, and re-layouts  3.95 us

profile of v1, /device:TPU:0, one launch (start us, length us, event | category | flops | bytes accessed | tf_op | source)
XLA Modules:
  0.0 123.1 jit_solution(5990444256172344007)
XLA Ops:
  0.6 118.5 %attn.1 = (bf16[768,128]{1,0:T(8,128)(2,1)}, bf16[768,128]{1,0:T(8,128)(2,1)}, bf16[192,128]{1,0:T(8,128)(2,1)}, bf16[192,128]{1,0:T(8,128)(2,1)}) custom-call(bf16[768,128]{1,0:T(8,128)(2,1)} %bitcast.10, bf16[192,128]{1,0:T(8,128)(2,1)} %bitcast.14, bf16[192,128]{1,0:T(8,128)(2,1)} %bitcast.15, bf16[768,128]{1,0:T(8,128)(2,1)} %bitcast.11), custom_call_target="tpu_custom_call" | custom-call | tf_op jit(solution)/shard_map/attn/pallas_call | solution.py:612
  119.1 0.0 copy-start
  119.1 1.7 %copy.12 = bf16[1,192,4,128]{3,2,1,0:T(4,128)(2,1)} copy(bf16[1,192,4,128]{3,2,1,0:T(4,128)(2,1)} %bitcast.9) | data formatting | bytes 393216
  120.8 0.0 copy-done
  120.8 0.0 copy-start.2
  120.8 0.7 copy.13
  121.5 0.1 copy-done.2
  121.6 0.0 copy-start.1
  121.6 0.6 copy.14
  122.2 0.2 copy-done.1
  122.4 0.6 copy.15
Async XLA Ops:
  119.1 1.7 %copy-start = (bf16[768,128]{1,0:T(8,128)(2,1)S(1)}, bf16[768,128]{1,0:T(8,128)(2,1)}, u32[]{:S(2)}) copy-start(bf16[768,128]{1,0:T(8,128)(2,1)} %get-tuple-element.9) | copy-start | bytes 589828
  120.8 0.8 copy-start.2
  121.6 0.8 copy-start.1

commit v2 on v1

v2 whole, which is shorter than its diff:
```python
import functools
import math
import jax
import jax.numpy as jnp
from jax import lax
from jax.experimental import pallas as pl
from jax.experimental.pallas import tpu as pltpu
from jax.sharding import PartitionSpec as P

CTX_AXES = ('ctxo', 'ctx')
MESH = pl.DeviceIdType.MESH
f32 = jnp.float32
bf16 = jnp.bfloat16
i32 = jnp.int32

ROWS = 768
HD = 128
SUB = 48
T = 256
NT = ROWS // T
SCALE = 1.0 / math.sqrt(HD)
SCALE2 = SCALE * math.log2(math.e)
NEG = -1e30
QUAD = 4
TRIO = 3
OFFS = (1, 2, 3)
TILES = range(NT)
N_FULL = 14


def dot(a, b, ca, cb):
    return lax.dot_general(a, b, (((ca,), (cb,)), ((), ())), preferred_element_type=f32)


def tile(n):
    return slice(n * T, (n + 1) * T)


def body(q_in, k_in, v_in, do_in, o_out, dq_out, dk_out, dv_out,
         q_all, do_all, k_all, v_all, kt, vt, ot, dqt, dk, dv, cache, scb, dpb, mx_run,
         m_run, l_run, lse, dd, stat_all,
         or1, or2, dqr1, dqr2, dkr1, dvr1, dk2, dv2, dkr2, dvr2, kst, vst, dk_fin, dv_fin,
         ka_ss, ka_rs, va_ss, va_rs, kx_ss, kx_rs, vy_ss, vy_rs, ky_ss, ky_rs, vx_ss, vx_rs,
         q_ss, q_rs, do_ss, do_rs, st_ss, st_rs, o1_ss, o1_rs, o2_ss, o2_rs,
         g1_ss, g1_rs, g2_ss, g2_rs, rk1_ss, rk1_rs, rv1_ss, rv1_rs, rk2_ss, rk2_rs, rv2_ss, rv2_rs,
         fk_ss, fk_rs, fv_ss, fv_rs):
    a = lax.axis_index('ctxo')
    b = lax.axis_index('ctx')
    z = b // 16
    y = (b // 4) % 4
    x = b % 4
    m_blk = 4 * y + x
    i_own = 4 * a + z
    pa = 1 - a
    par = (a + z) % 2

    def dev(a_, z_, y_, x_):
        return {'ctxo': a_, 'ctx': 16 * z_ + 4 * y_ + x_}

    def rc(src, dst, ss, rs, to):
        return pltpu.make_async_remote_copy(src_ref=src, dst_ref=dst, send_sem=ss, recv_sem=rs, device_id=to, device_id_type=MESH)

    partner = dev(pa, z, y, x)

    def got(ref, ss, rs):
        rc(ref, ref, ss, rs, partner).wait_recv()

    def sent(ref, ss, rs):
        rc(ref, ref, ss, rs, partner).wait_send()

    def zpeer(d):
        return (z + d) % 4

    def sub_rows(n):
        return pl.ds(pl.multiple_of(SUB * n, SUB), SUB)

    def group_of(s):
        a_s = s // 2
        return a_s, 2 * (s % 2) + (a_s + a) % 2

    bar = pltpu.get_barrier_semaphore()

    def hello(to):
        pl.semaphore_signal(bar, inc=1, device_id=to, device_id_type=MESH)

    hello(partner)
    for d in OFFS:
        hello(dev(a, zpeer(d), y, x))
        hello(dev(pa, zpeer(d), y, x))
        hello(dev(a, z, (y + d) % QUAD, x))
        hello(dev(a, z, y, (x + d) % QUAD))
    pl.semaphore_wait(bar, 13)

    k5 = k_all.reshape(4, 4, 4, SUB, HD)
    v5 = v_all.reshape(4, 4, 4, SUB, HD)

    s_me = 2 * a + z // 2
    keep = par == a
    for d in range(QUAD):
        rows = sub_rows(zpeer(d))
        kc = rc(k_in.at[rows], k5.at[s_me, y, x], ka_ss.at[d], ka_rs.at[s_me], dev(par, zpeer(d), y, x))
        vc = rc(v_in.at[rows], v5.at[s_me, y, x], va_ss.at[d], va_rs.at[s_me], dev(par, zpeer(d), y, x))
        if d == 0:
            @pl.when(keep)
            def _():
                k_all[s_me, sub_rows(m_blk), :] = k_in[rows, :]
                v_all[s_me, sub_rows(m_blk), :] = v_in[rows, :]

            @pl.when(jnp.logical_not(keep))
            def _():
                kc.start()
                vc.start()
        else:
            kc.start()
            vc.start()

    rc(q_in, q_all.at[i_own], q_ss.at[0], q_rs.at[i_own], partner).start()
    for d in OFFS:
        rc(q_in, q_all.at[i_own], q_ss.at[d], q_rs.at[i_own], dev(a, zpeer(d), y, x)).start()
    q_all[i_own] = q_in[...]
    do_all[i_own] = do_in[...]
    dk[...] = jnp.zeros(dk.shape, f32)
    dv[...] = jnp.zeros(dv.shape, f32)

    def kv_share():
        for s in range(QUAD):
            a_s, z_s = group_of(s)

            @pl.when(jnp.logical_not((a_s == a) & (z_s == z)))
            def _():
                got(k5.at[s, y, x], ka_ss.at[0], ka_rs.at[s])
                got(v5.at[s, y, x], va_ss.at[0], va_rs.at[s])
        for d in OFFS:
            rc(k5.at[:, y, x], k5.at[:, y, x], kx_ss.at[d - 1], kx_rs.at[d - 1], dev(a, z, y, (x + d) % QUAD)).start()
            rc(v5.at[:, y, x], v5.at[:, y, x], vy_ss.at[d - 1], vy_rs.at[d - 1], dev(a, z, (y + d) % QUAD, x)).start()

    def kv_spread():
        for d in OFFS:
            got(k5.at[:, y, (x - d) % QUAD], kx_ss.at[d - 1], kx_rs.at[d - 1])
            got(v5.at[:, (y - d) % QUAD, x], vy_ss.at[d - 1], vy_rs.at[d - 1])
        for s in range(QUAD):
            for d in OFFS:
                rc(k5.at[s, y], k5.at[s, y], ky_ss.at[s, d - 1], ky_rs.at[s, d - 1], dev(a, z, (y + d) % QUAD, x)).start()
                rc(v5.at[s, :, x], v5.at[s, :, x], vx_ss.at[s, d - 1], vx_rs.at[s, d - 1], dev(a, z, y, (x + d) % QUAD)).start()

    def kv_ready(s):
        for d in OFFS:
            got(k5.at[s, (y - d) % QUAD], ky_ss.at[s, d - 1], ky_rs.at[s, d - 1])
            got(v5.at[s, :, (x - d) % QUAD], vx_ss.at[s, d - 1], vx_rs.at[s, d - 1])
        kt[s] = k_all[s].T
        vt[s] = v_all[s].T

    kv_share()
    dqt[...] = jnp.zeros(dqt.shape, f32)
    ot[...] = jnp.zeros(ot.shape, f32)
    kv_spread()
    rc(do_in, do_all.at[i_own], do_ss.at[0], do_rs.at[i_own], partner).start()
    for d in OFFS:
        rc(do_in, do_all.at[i_own], do_ss.at[d], do_rs.at[i_own], dev(a, zpeer(d), y, x)).start()
    m_run[...] = jnp.full(m_run.shape, NEG, f32)
    l_run[...] = jnp.zeros(l_run.shape, f32)

    def hand_on(full, ss, rs, d):
        i_r = 4 * a + (z - d) % QUAD
        got(full.at[i_r], ss.at[0], rs.at[i_r])
        rc(full.at[i_r], full.at[i_r], ss.at[3 + d], rs.at[i_r], partner).start()

    def q_ready(d):
        i_r = 4 * pa + (z - d) % QUAD
        got(q_all.at[i_r], q_ss.at[0], q_rs.at[i_r])

    hand_on(q_all, q_ss, q_rs, 1)
    hand_on(q_all, q_ss, q_rs, 3)

    def g_of(s):
        a_s, z_s = group_of(s)
        return 4 * a_s + z_s

    def full_count(i):
        n = jnp.int32(0)
        for s in range(QUAD):
            n = n + (g_of(s) < i).astype(i32)
        return n

    def cache_at(i, s):
        n = i - g_of(s) - 1
        for r in OFFS:
            n = n + (r <= s) * (7 - g_of(r - 1))
        return n

    def seen(j, ct):
        key_id = j * T + lax.broadcasted_iota(i32, (T, T), 0)
        pos = (ct * T + lax.broadcasted_iota(i32, (1, T), 1)) // 4
        last = SUB * m_blk + jnp.clip(pos - SUB * z, -1, SUB - 1)
        return key_id <= last

    def rsum(p):
        return jnp.sum(p.reshape(p.shape[0] // 8, 8, p.shape[1]), axis=0)

    def rmax(p):
        return jnp.max(p.reshape(p.shape[0] // 8, 8, p.shape[1]), axis=0)

    def fwd_scores(i, s, pc, ct, j, mx, masked=False):
        t = dot(k_all[s, tile(j), :], q_all[i, tile(ct), :], 1, 1) * SCALE2
        if masked:
            t = jnp.where(seen(j, ct), t, -jnp.inf)
        cache[pc, tile(j), tile(ct)] = t
        r = rmax(t)
        return r if mx is None else jnp.maximum(mx, r)

    def fwd_pair(i, s, pc, mx, i_n, pc_n, masked=False):
        for ct in TILES:
            cs = tile(ct)
            last = ct == NT - 1
            nxt = (i_n, s, pc_n, 0) if last else (i, s, pc, ct + 1)
            m_old = m_run[i, :, cs]
            m_new = jnp.maximum(m_old, jnp.max(mx, axis=0, keepdims=True))
            al = jnp.exp2(m_old - m_new)
            mx = None
            lp = None
            o = None
            for j in TILES:
                if not (masked and last):
                    mx = fwd_scores(*nxt, j, mx, masked)
                p = jnp.exp2(cache[pc, tile(j), cs] - m_new)
                r = rsum(p)
                lp = r if lp is None else lp + r
                oj = dot(vt[s, :, tile(j)], p.astype(bf16), 1, 0)
                o = oj if o is None else o + oj
            l_run[i, :, cs] = l_run[i, :, cs] * al + jnp.sum(lp, axis=0, keepdims=True)
            ot[i, :, cs] = ot[i, :, cs] * al + o
            m_run[i, :, cs] = m_new
        return mx

    def nth(t):
        r = t // 2
        d = r + (r >= 2) * (1 - 2 * (r - 2))
        return 4 * ((a + t) % 2) + (z + d) % QUAD

    def fwd_slot(s):
        kv_ready(s)
        g = g_of(s)

        def after(t):
            n = jnp.int32(8)
            for k in range(7, -1, -1):
                n = jnp.where((k > t) & (nth(k) > g), k, n)
            return n

        @pl.when(s == 0)
        def _():
            for d in (0, 1, 3):
                q_ready(d)
        t0 = after(jnp.int32(-1))

        @pl.when(t0 < 8)
        def _():
            mx = None
            for j in TILES:
                mx = fwd_scores(nth(t0), s, cache_at(nth(t0), s), 0, j, mx)
            mx_run[...] = mx

        def pair(t, c):
            @pl.when((s == 0) & (t == 3))
            def _():
                hand_on(q_all, q_ss, q_rs, 2)

            @pl.when((s == 0) & (t == 5))
            def _():
                q_ready(2)

            @pl.when(nth(t) > g)
            def _():
                i = nth(t)
                t_n = after(t)
                i_n = jnp.where(t_n < 8, nth(t_n), i)
                mx_run[...] = fwd_pair(i, s, cache_at(i, s), mx_run[...], i_n, cache_at(i_n, s))
            return c
        lax.fori_loop(0, 8, pair, 0)
        mx = None
        for j in TILES:
            mx = fwd_scores(g, s, N_FULL, 0, j, mx, True)
        fwd_pair(g, s, N_FULL, mx, None, None, True)

    def stat_peer(off, sign):
        da, dz = divmod(off, 4)
        return (a + da) % 2, (z + sign * dz) % QUAD

    def fwd_done(i, c):
        a_i = i // 4
        z_i = i % QUAD

        @pl.when(a_i != a)
        def _():
            got(do_all.at[i], do_ss.at[0], do_rs.at[i])
        d_part = jnp.sum(do_all[i].T.astype(f32) * ot[i], axis=0, keepdims=True)
        stat_all[i, i_own, 0:1, :] = m_run[i]
        stat_all[i, i_own, 1:2, :] = l_run[i]
        stat_all[i, i_own, 2:3, :] = d_part
        for off in range(1, 8):
            at, zt = stat_peer(off, 1)
            rc(stat_all.at[i, i_own], stat_all.at[i, i_own], st_ss.at[i, off - 1], st_rs.at[i, off - 1], dev(at, zt, y, x)).start()

        @pl.when(a_i != a)
        def _():
            rc(ot.at[i], or1.at[z_i], o1_ss.at[z_i], o1_rs.at[z_i], partner).start()
        return c

    def pair_max(i, z_):
        return jnp.maximum(stat_all[i, z_, 0:1, :], stat_all[i, 4 + z_, 0:1, :])

    def out_join(z_o):
        i = 4 * a + z_o
        got(or1.at[z_o], o1_ss.at[z_o], o1_rs.at[z_o])
        got(stat_all.at[i, 4 * pa + z], st_ss.at[i, 3], st_rs.at[i, 3])
        top = pair_max(i, z)
        w_own = jnp.exp2(stat_all[i, i_own, 0:1, :] - top)
        w_par = jnp.exp2(stat_all[i, 4 * pa + z, 0:1, :] - top)
        for ct in TILES:
            cs = tile(ct)
            ot[i, :, cs] = ot[i, :, cs] * w_own[:, cs] + or1[z_o, :, cs] * w_par[:, cs]

        @pl.when(z_o != z)
        def _():
            h = (z_o - z) % QUAD - 1
            rc(ot.at[i], or2.at[h], o2_ss.at[z_o], o2_rs.at[h], dev(a, z_o, y, x)).start()

    def slot_step(s, c):
        fwd_slot(s)

        @pl.when(s == 1)
        def _():
            for d in (1, 3, 2):
                hand_on(do_all, do_ss, do_rs, d)

        @pl.when(s == 2)
        def _():
            lax.fori_loop(0, g_of(3), fwd_done, 0)

        @pl.when(s == 3)
        def _():
            lax.fori_loop(g_of(3), 8, fwd_done, 0)
        return c
    lax.fori_loop(0, 4, slot_step, 0)

    def row_max(i):
        big = stat_all[i, 0, 0:1, :]
        for k in range(1, 8):
            big = jnp.maximum(big, stat_all[i, k, 0:1, :])
        return big

    def stats(i):
        for off in range(1, 8):
            af, zf = stat_peer(off, -1)

            def take():
                got(stat_all.at[i, 4 * af + zf], st_ss.at[i, off - 1], st_rs.at[i, off - 1])
            if off == 4:
                pl.when(i // 4 != a)(take)
            else:
                take()
        big = row_max(i)
        tot = jnp.zeros((1, ROWS), f32)
        dsum = jnp.zeros((1, ROWS), f32)
        for k in range(8):
            w = jnp.exp2(stat_all[i, k, 0:1, :] - big)
            tot = tot + w * stat_all[i, k, 1:2, :]
            dsum = dsum + w * stat_all[i, k, 2:3, :]
        lse[i] = big + jnp.log(tot) * math.log2(math.e)
        dd[i] = dsum / tot

    def dq_join(z_o):
        i = 4 * a + z_o
        got(dqr1.at[z_o], g1_ss.at[z_o], g1_rs.at[z_o])
        for ct in TILES:
            cs = tile(ct)
            dqt[i, :, cs] = dqt[i, :, cs] + dqr1[z_o, :, cs]

        @pl.when(z_o != z)
        def _():
            h = (z_o - z) % 4 - 1
            rc(dqt.at[i], dqr2.at[h], g2_ss.at[z_o], g2_rs.at[h], dev(a, z_o, y, x)).start()

    def bwd_scores(i, s, u, masked):
        j, ct = divmod(u, NT)
        dpb[u % TRIO] = dot(v_all[s, tile(j), :], do_all[i, tile(ct), :], 1, 1)
        if masked:
            t = dot(k_all[s, tile(j), :], q_all[i, tile(ct), :], 1, 1) * SCALE2
            scb[u % TRIO] = jnp.where(seen(j, ct), t, -jnp.inf)

    def bwd_pair(i, s, pc, s_n, masked=False):
        acc_v = None
        acc_k = None
        pend = None

        def products(u, p, ds, acc_v, acc_k):
            j, ct = divmod(u, NT)
            e = dot(p, do_all[i, tile(ct), :], 1, 0)
            g = dot(ds, q_all[i, tile(ct), :], 1, 0)
            acc_v = e if ct == 0 else acc_v + e
            acc_k = g if ct == 0 else acc_k + g
            dqt[i, :, tile(ct)] += dot(kt[s, :, tile(j)], ds, 1, 0)
            if ct == NT - 1:
                dv[s, tile(j), :] += acc_v
                dk[s, tile(j), :] += acc_k
            return acc_v, acc_k

        n_u = NT * NT
        for u in range(n_u):
            j, ct = divmod(u, NT)
            if u < n_u - 1:
                bwd_scores(i, s, u + 1, masked)
            else:
                bwd_scores(i, s_n, 0, False)
            t = scb[u % TRIO] if masked else cache[pc, tile(j), tile(ct)]
            p = jnp.exp2(t - lse[i, :, tile(ct)])
            ds = p * (dpb[u % TRIO] - dd[i, :, tile(ct)])
            now = p.astype(bf16), ds.astype(bf16)
            if pend is not None:
                acc_v, acc_k = products(u - 1, *pend, acc_v, acc_k)
            pend = now
        products(n_u - 1, *pend, acc_v, acc_k)

    def bwd_block(i):
        n_i = full_count(i)
        diag = (i // 4 + i) % 2 == a
        s_d = 2 * (i // 4) + i % QUAD // 2

        @pl.when(diag)
        def _():
            bwd_scores(i, s_d, 0, True)
            bwd_pair(i, s_d, N_FULL, 0, True)

        @pl.when(jnp.logical_not(diag))
        def _():
            bwd_scores(i, 0, 0, False)

        def pair(s, c):
            bwd_pair(i, s, cache_at(i, s), jnp.minimum(s + 1, 3))
            return c
        lax.fori_loop(0, n_i, pair, 0)

    dk5 = dk.reshape(4, 4, 4, SUB, HD)
    dv5 = dv.reshape(4, 4, 4, SUB, HD)
    dkr14 = dkr1.reshape(4, 3, 4, SUB, HD)
    dvr14 = dvr1.reshape(4, 3, 4, SUB, HD)
    dk24 = dk2.reshape(4, 4, SUB, HD)
    dv24 = dv2.reshape(4, 4, SUB, HD)

    def kv_first(s):
        for d in OFFS:
            yt = (y + d) % 4
            xt = (x + d) % 4
            rc(dk5.at[s, yt], dkr14.at[s, d - 1], rk1_ss.at[s, d - 1], rk1_rs.at[s, d - 1], dev(a, z, yt, x)).start()
            rc(dv5.at[s, :, xt], dvr14.at[s, d - 1], rv1_ss.at[s, d - 1], rv1_rs.at[s, d - 1], dev(a, z, y, xt)).start()

    def kv_second(s):
        for d in OFFS:
            got(dkr14.at[s, d - 1], rk1_ss.at[s, d - 1], rk1_rs.at[s, d - 1])
            got(dvr14.at[s, d - 1], rv1_ss.at[s, d - 1], rv1_rs.at[s, d - 1])
        tot = dk[s, pl.ds(pl.multiple_of(4 * SUB * y, 4 * SUB), 4 * SUB), :]
        for d in range(TRIO):
            tot = tot + dkr1[s, d]
        dk2[s] = tot
        for n in range(QUAD):
            tot = dv[s, sub_rows(4 * n + x), :]
            for d in range(TRIO):
                tot = tot + dvr1[s, d, n * SUB:(n + 1) * SUB, :]
            dv2[s, n * SUB:(n + 1) * SUB, :] = tot
        for d in OFFS:
            yt = (y + d) % 4
            xt = (x + d) % 4
            rc(dk24.at[s, xt], dkr2.at[s, d - 1], rk2_ss.at[s, d - 1], rk2_rs.at[s, d - 1], dev(a, z, y, xt)).start()
            rc(dv24.at[s, yt], dvr2.at[s, d - 1], rv2_ss.at[s, d - 1], rv2_rs.at[s, d - 1], dev(a, z, yt, x)).start()

    def kv_third(s):
        for d in OFFS:
            got(dkr2.at[s, d - 1], rk2_ss.at[s, d - 1], rk2_rs.at[s, d - 1])
            got(dvr2.at[s, d - 1], rv2_ss.at[s, d - 1], rv2_rs.at[s, d - 1])
        tk = dk2[s, sub_rows(x), :]
        tv = dv2[s, sub_rows(y), :]
        for d in range(TRIO):
            tk = tk + dkr2[s, d]
            tv = tv + dvr2[s, d]
        kst[s] = (tk * SCALE).astype(bf16)
        vst[s] = tv.astype(bf16)
        a_s, z_s = group_of(s)
        mine = (a_s == a) & (z_s == z)
        h = (z_s - z) % 4
        rows = sub_rows(z)

        @pl.when(mine)
        def _():
            dk_fin[rows, :] = kst[s]
            dv_fin[rows, :] = vst[s]

        @pl.when(jnp.logical_not(mine))
        def _():
            rc(kst.at[s], dk_fin.at[rows], fk_ss.at[s], fk_rs.at[h], dev(a_s, z_s, y, x)).start()
            rc(vst.at[s], dv_fin.at[rows], fv_ss.at[s], fv_rs.at[h], dev(a_s, z_s, y, x)).start()

    def on_slots(n, delay, fn, late):
        for s in range(QUAD):
            when = (7, 5, 3, 1)[s] + a * ((6, 5, 4, 2)[s] - (7, 5, 3, 1)[s]) + delay
            pl.when((when == n) | ((n == 8) & (when > 7)) if late else when == n)(functools.partial(fn, s))

    def bwd_step(n, c):
        i = 7 - n + ((n >= 1) & (n <= 4)).astype(i32) - 4 * (n == 0).astype(i32)
        a_i = i // 4
        z_i = i % QUAD
        stats(i)
        bwd_block(i)

        @pl.when(a_i != a)
        def _():
            rc(dqt.at[i], dqr1.at[z_i], g1_ss.at[z_i], g1_rs.at[z_i], partner).start()
        on_slots(n, 0, kv_first, False)

        @pl.when((n == 0) & (a == 1))
        def _():
            out_join(3)
            out_join(2)

        @pl.when(((a == 0) & (n == 1)) | ((a == 1) & (n == 2)))
        def _():
            dq_join(3)

        @pl.when(((a == 0) & (n == 6)) | ((a == 1) & (n == 3)))
        def _():
            dq_join(2)

        @pl.when(((a == 0) & (n == 7)) | ((a == 1) & (n == 4)))
        def _():
            dq_join(1)

        @pl.when((a == 1) & (n == 5))
        def _():
            dq_join(0)
        on_slots(n, 2, kv_second, False)
        on_slots(n, 4, kv_third, False)
        return c

    @pl.when(a == 0)
    def _():
        for n in (3, 2, 1, 0):
            out_join(n)

    @pl.when(a == 1)
    def _():
        out_join(1)
        out_join(0)
    lax.fori_loop(0, 8, bwd_step, 0)

    @pl.when(a == 0)
    def _():
        dq_join(0)

    for h in range(TRIO):
        got(or2.at[h], o2_ss.at[0], o2_rs.at[h])
    w_z = [jnp.exp2(pair_max(i_own, (z - h) % QUAD) - lse[i_own]) for h in range(QUAD)]
    for ct in TILES:
        cs = tile(ct)
        o = ot[i_own, :, cs] * w_z[0][:, cs]
        for h in OFFS:
            o = o + or2[h - 1, :, cs] * w_z[h][:, cs]
        o_out[cs, :] = o.T.astype(bf16)
    on_slots(8, 2, kv_second, True)
    on_slots(8, 4, kv_third, True)
    for h in range(TRIO):
        got(dqr2.at[h], g2_ss.at[0], g2_rs.at[h])
    for ct in TILES:
        cs = tile(ct)
        dq_out[cs, :] = ((dqt[i_own, :, cs] + dqr2[0, :, cs] + dqr2[1, :, cs] + dqr2[2, :, cs]).T * SCALE).astype(bf16)
    for h in range(QUAD):
        rows = sub_rows((z - h) % 4)

        def take():
            got(dk_fin.at[rows], fk_ss.at[0], fk_rs.at[h])
            got(dv_fin.at[rows], fv_ss.at[0], fv_rs.at[h])
        if h == 0:
            pl.when(jnp.logical_not(keep))(take)
        else:
            take()
    dk_out[...] = dk_fin[...]
    dv_out[...] = dv_fin[...]

    rows0 = pl.ds(0, SUB)
    for d in range(QUAD):
        def left():
            sent(k_in.at[rows0], ka_ss.at[d], ka_rs.at[0])
            sent(v_in.at[rows0], va_ss.at[d], va_rs.at[0])
        if d == 0:
            pl.when(jnp.logical_not(keep))(left)
        else:
            left()
        for h in range(TRIO):
            sent(k5.at[d, y], ky_ss.at[d, h], ky_rs.at[d, h])
            sent(v5.at[d, :, x], vx_ss.at[d, h], vx_rs.at[d, h])
    for d in range(TRIO):
        sent(k5.at[:, y, x], kx_ss.at[d], kx_rs.at[d])
        sent(v5.at[:, y, x], vy_ss.at[d], vy_rs.at[d])
    for d in range(7):
        sent(q_in, q_ss.at[d], q_rs.at[0])
        sent(do_in, do_ss.at[d], do_rs.at[0])

    def drain_i(i, c):
        for off in range(7):
            sent(stat_all.at[i, i_own], st_ss.at[i, off], st_rs.at[i, off])
        return c
    lax.fori_loop(0, 8, drain_i, 0)
    for n in range(QUAD):
        sent(ot.at[n], o1_ss.at[n], o1_rs.at[n])
        sent(ot.at[n], g1_ss.at[n], g1_rs.at[n])

        @pl.when(n != z)
        def _():
            sent(ot.at[n], o2_ss.at[n], o2_rs.at[0])
            sent(ot.at[n], g2_ss.at[n], g2_rs.at[0])
        for d in range(TRIO):
            sent(dkr14.at[0, 0], rk1_ss.at[n, d], rk1_rs.at[n, d])
            sent(dvr14.at[0, 0], rv1_ss.at[n, d], rv1_rs.at[n, d])
            sent(dkr2.at[0, 0], rk2_ss.at[n, d], rk2_rs.at[n, d])
            sent(dvr2.at[0, 0], rv2_ss.at[n, d], rv2_rs.at[n, d])
        a_s, z_s = group_of(n)

        @pl.when(jnp.logical_not((a_s == a) & (z_s == z)))
        def _():
            sent(kst.at[n], fk_ss.at[n], fk_rs.at[0])
            sent(vst.at[n], fv_ss.at[n], fv_rs.at[0])


def solution(mesh):
    blk_spec = P('data', CTX_AXES, None, None)

    def v(shape, dtype):
        return pltpu.VMEM(shape, dtype)

    def sem(*shape):
        return pltpu.SemaphoreType.DMA(shape)

    big = (ROWS, HD)
    scratch = [
        v((8,) + big, bf16), v((8,) + big, bf16),
        v((4,) + big, bf16), v((4,) + big, bf16),
        v((4, HD, ROWS), bf16), v((4, HD, ROWS), bf16),
        v((8, HD, ROWS), f32), v((8, HD, ROWS), f32),
        v((4,) + big, f32), v((4,) + big, f32),
        v((N_FULL + 1, ROWS, ROWS), f32),
        v((3, T, T), f32), v((3, T, T), f32),
        v((8, T), f32),
        v((8, 1, ROWS), f32), v((8, 1, ROWS), f32), v((8, 1, ROWS), f32), v((8, 1, ROWS), f32),
        v((8, 8, 3, ROWS), f32),
        v((4, HD, ROWS), f32), v((3, HD, ROWS), f32), v((4, HD, ROWS), f32), v((3, HD, ROWS), f32),
        v((4, 3, 4 * SUB, HD), f32), v((4, 3, 4 * SUB, HD), f32),
        v((4, 4 * SUB, HD), f32), v((4, 4 * SUB, HD), f32),
        v((4, 3, SUB, HD), f32), v((4, 3, SUB, HD), f32),
        v((4, SUB, HD), bf16), v((4, SUB, HD), bf16),
        v((4 * SUB, HD), bf16), v((4 * SUB, HD), bf16),
        *[sem(QUAD)] * 4, *[sem(TRIO)] * 4, *[sem(QUAD, TRIO)] * 4,
        *[sem(7), sem(8)] * 2, *[sem(8, 7)] * 2,
        *[sem(QUAD), sem(QUAD), sem(QUAD), sem(TRIO)] * 2,
        *[sem(QUAD, TRIO)] * 8, *[sem(QUAD)] * 4,
    ]
    call = pl.pallas_call(
        body,
        name='attn',
        out_shape=[jax.ShapeDtypeStruct(big, bf16), jax.ShapeDtypeStruct(big, bf16),
                   jax.ShapeDtypeStruct((4 * SUB, HD), bf16), jax.ShapeDtypeStruct((4 * SUB, HD), bf16)],
        in_specs=[pl.BlockSpec(memory_space=pltpu.VMEM)] * 4,
        out_specs=[pl.BlockSpec(memory_space=pltpu.VMEM)] * 4,
        scratch_shapes=scratch,
        compiler_params=pltpu.CompilerParams(collective_id=0, has_side_effects=True, vmem_limit_bytes=67043328),
    )

    def local_attn(q_in, k_in, v_in, do_in):
        o, dq, dk, dv = call(q_in.reshape(big), k_in.reshape(4 * SUB, HD), v_in.reshape(4 * SUB, HD), do_in.reshape(big))
        return o.reshape(q_in.shape), dq.reshape(q_in.shape), dk.reshape(k_in.shape), dv.reshape(k_in.shape)

    return jax.shard_map(local_attn, mesh=mesh, in_specs=(blk_spec,) * 4, out_specs=(blk_spec,) * 4, check_vma=False)
```

time: 123 us -> 105 us (0.85)
  Pallas kernels: 118 us -> 99.4 us
    pallas_call x1, Pallas kernels: 118 us -> 99.4 us  [local_attn(): call(q_in.reshape(big), k_in.reshape(4 * SUB, HD), v_in.reshape(4 * SUB,...]
where the time goes in v2:
time: 105 us; the launch traced here: 104 us
  Pallas kernels  99.4 us (95%)
  local copies, waits for them, and re-layouts  3.95 us (4%)
    pallas_call x1, Pallas kernels, local_attn(): call(q_in.reshape(big), k_in.reshape(4 * SUB, HD), v_in.reshape(4 * SUB,...  99.4 us
    unnamed x10, local copies, waits for them, and re-layouts  3.95 us

profile of v2, /device:TPU:0, one launch (start us, length us, event | category | flops | bytes accessed | tf_op | source)
XLA Modules:
  0.0 104.0 jit_solution(4644483780975931682)
XLA Ops:
  0.6 99.4 %attn.1 = (bf16[768,128]{1,0:T(8,128)(2,1)}, bf16[768,128]{1,0:T(8,128)(2,1)}, bf16[192,128]{1,0:T(8,128)(2,1)}, bf16[192,128]{1,0:T(8,128)(2,1)}) custom-call(bf16[768,128]{1,0:T(8,128)(2,1)} %bitcast.10, bf16[192,128]{1,0:T(8,128)(2,1)} %bitcast.14, bf16[192,128]{1,0:T(8,128)(2,1)} %bitcast.15, bf16[768,128]{1,0:T(8,128)(2,1)} %bitcast.11), custom_call_target="tpu_custom_call" | custom-call | tf_op jit(solution)/shard_map/attn/pallas_call | solution.py:676
  100.0 0.0 copy-start
  100.0 1.7 %copy.12 = bf16[1,192,4,128]{3,2,1,0:T(4,128)(2,1)} copy(bf16[1,192,4,128]{3,2,1,0:T(4,128)(2,1)} %bitcast.9) | data formatting | bytes 393216
  101.7 0.0 copy-done
  101.7 0.0 copy-start.2
  101.7 0.7 copy.13
  102.4 0.1 copy-done.2
  102.5 0.0 copy-start.1
  102.5 0.6 copy.14
  103.2 0.2 copy-done.1
  103.4 0.6 copy.15
Async XLA Ops:
  100.0 1.7 %copy-start = (bf16[768,128]{1,0:T(8,128)(2,1)S(1)}, bf16[768,128]{1,0:T(8,128)(2,1)}, u32[]{:S(2)}) copy-start(bf16[768,128]{1,0:T(8,128)(2,1)} %get-tuple-element.9) | copy-start | bytes 589828
  101.7 0.8 copy-start.2
  102.5 0.8 copy-start.1

commit v3 on v0

v3 whole, which is shorter than its diff:
```python
import functools
import math
import jax
import jax.numpy as jnp
from jax import lax
from jax.experimental import pallas as pl
from jax.experimental.pallas import tpu as pltpu
from jax.sharding import PartitionSpec as P

CTX_AXES = ('ctxo', 'ctx')
MESH = pl.DeviceIdType.MESH
f32 = jnp.float32
bf16 = jnp.bfloat16
i32 = jnp.int32

Z = 4
G = 8
HD = 128
SUB = 48
BLK = Z * SUB
ROWS = Z * BLK
HALF = ROWS // 2
T = 256
NT = ROWS // T
TILES = range(NT)
QUAD = range(Z)
OFFS = (1, 2, 3)
NEAR = (1, 3)
SCALE = 1.0 / math.sqrt(HD)
SCALE2 = SCALE * math.log2(math.e)
NEG = -1e30
N_FULL = 14
LAST = G - 1

KINDS = (('ka', Z), ('va', Z), ('kx', Z), ('vy', Z), ('ky', Z * Z), ('vx', Z * Z),
         ('q', G), ('qh', Z), ('qf', Z), ('do', G), ('doh', Z), ('dof', Z), ('in', Z),
         ('st', Z), ('sz', Z * Z), ('ld', G), ('o', Z), ('oz', Z), ('g', Z), ('gz', Z),
         ('rk', Z * Z), ('rv', Z * Z), ('sk', Z * Z), ('sv', Z * Z), ('fk', Z), ('fv', Z))
N_SEM = sum(n for _, n in KINDS)


def dot(a, b, ca, cb):
    return lax.dot_general(a, b, (((ca,), (cb,)), ((), ())), preferred_element_type=f32)


def tile(n):
    return slice(n * T, (n + 1) * T)


def rem(n, k=Z):
    return n % k if isinstance(n, int) else lax.rem(n, jnp.int32(k))


def div(n, k=Z):
    return n // k if isinstance(n, int) else lax.div(n, jnp.int32(k))


def sub_rows(n):
    return pl.ds(pl.multiple_of(SUB * n, SUB), SUB)


def body(q_hbm, k_hbm, v_hbm, do_hbm, o_out, dq_out, dk_out, dv_out,
         k_loc, v_loc, q_all, do_all, k_all, v_all, kt, vt, ot, dqt, dk, dv, cache, scb, dpb, mx_run,
         m_run, l_run, st_loc, st_par, st_col, ld,
         or1, or2, dqr1, dqr2, dkr1, dvr1, dk2, dv2, dkr2, dvr2, kst, vst, dk_fin, dv_fin, s_sem, r_sem):
    a = lax.axis_index('ctxo')
    b = lax.axis_index('ctx')
    z = div(b, Z * Z)
    y = rem(div(b))
    x = rem(b)
    m_blk = Z * y + x
    i_own = Z * a + z
    pa = 1 - a
    par = rem(a + z, 2)
    base = {}
    for kind, n in KINDS:
        base[kind] = sum(base[p][1] for p in base), n

    def dev(a_, z_, y_, x_):
        return {'ctxo': a_, 'ctx': Z * Z * z_ + Z * y_ + x_}

    partner = dev(pa, z, y, x)

    def col(d):
        return dev(a, rem(z + d), y, x)

    def other_col(d):
        return dev(pa, rem(z + d), y, x)

    def in_y(d):
        return dev(a, z, rem(y + d), x)

    def in_x(d):
        return dev(a, z, y, rem(x + d))

    def rc(kind, n_s, n_r, src, dst, to):
        off = base[kind][0]
        return pltpu.make_async_remote_copy(src_ref=src, dst_ref=dst, send_sem=s_sem.at[off + n_s], recv_sem=r_sem.at[off + n_r],
                                            device_id=to, device_id_type=MESH)

    def send(kind, n_s, n_r, src, dst, to):
        rc(kind, n_s, n_r, src, dst, to).start()

    def got(kind, n, ref):
        rc(kind, n, n, ref, ref, partner).wait_recv()

    def sent(kind, n, ref):
        rc(kind, n, n, ref, ref, partner).wait_send()

    def when(cond, fn, *args):
        pl.when(cond)(functools.partial(fn, *args))

    def group_of(s):
        a_s = div(s, 2)
        return a_s, 2 * rem(s, 2) + rem(a_s + a, 2)

    def g_of(s):
        a_s, z_s = group_of(s)
        return Z * a_s + z_s

    def not_mine(s):
        return g_of(s) != i_own

    own = [(q_hbm, q_all.at[i_own]), (do_hbm, do_all.at[i_own]), (k_hbm, k_loc), (v_hbm, v_loc)]
    own = [pltpu.make_async_copy(src, dst, s_sem.at[base['in'][0] + n]) for n, (src, dst) in enumerate(own)]
    for c in reversed(own):
        c.start()
    bar = pltpu.get_barrier_semaphore()
    peers = [partner] + [f(d) for d in OFFS for f in (col, other_col, in_y, in_x)]
    for to in peers:
        pl.semaphore_signal(bar, inc=1, device_id=to, device_id_type=MESH)
    for c in reversed(own):
        c.wait()
    pl.semaphore_wait(bar, len(peers))

    k5 = k_all.reshape(Z, Z, Z, SUB, HD)
    v5 = v_all.reshape(Z, Z, Z, SUB, HD)

    s_me = 2 * a + div(z, 2)
    keep = par == a
    for d in QUAD:
        rows = sub_rows(rem(z + d))
        to = dev(par, rem(z + d), y, x)

        def give():
            send('ka', d, s_me, k_loc.at[rows], k5.at[s_me, y, x], to)
            send('va', d, s_me, v_loc.at[rows], v5.at[s_me, y, x], to)

        if d:
            give()
        else:
            @pl.when(keep)
            def _():
                k_all[s_me, sub_rows(m_blk), :] = k_loc[rows, :]
                v_all[s_me, sub_rows(m_blk), :] = v_loc[rows, :]
            when(jnp.logical_not(keep), give)
    send('q', i_own, i_own, q_all.at[i_own], q_all.at[i_own], partner)
    send('do', i_own, i_own, do_all.at[i_own], do_all.at[i_own], partner)
    dk[...] = jnp.zeros(dk.shape, f32)
    dv[...] = jnp.zeros(dv.shape, f32)

    def kv_share():
        for s in QUAD:
            @pl.when(not_mine(s))
            def _():
                got('ka', s, k5.at[s, y, x])
                got('va', s, v5.at[s, y, x])
        for d in OFFS:
            send('kx', d, d, k5.at[:, y, x], k5.at[:, y, x], in_x(d))
            send('vy', d, d, v5.at[:, y, x], v5.at[:, y, x], in_y(d))

    def kv_spread():
        for d in OFFS:
            got('kx', d, k5.at[:, y, rem(x + Z - d)])
            got('vy', d, v5.at[:, rem(y + Z - d), x])
        for s in QUAD:
            for d in OFFS:
                n = Z * s + d
                send('ky', n, n, k5.at[s, y], k5.at[s, y], in_y(d))
                send('vx', n, n, v5.at[s, :, x], v5.at[s, :, x], in_x(d))

    def kv_ready(s):
        for d in OFFS:
            got('ky', Z * s + d, k5.at[s, rem(y + Z - d)])
            got('vx', Z * s + d, v5.at[s, :, rem(x + Z - d)])
        kt[s] = k_all[s].T
        vt[s] = v_all[s].T

    def half(ref, h):
        return ref.at[pl.ds(h * HALF, HALF)]

    def near_send(kind, full):
        for d in NEAR:
            send(kind, rem(i_own + d, G), i_own, full.at[i_own], full.at[i_own], col(d))

    def pass_on(kind, full, i_r, n):
        send(kind + 'f', n, rem(i_r), full.at[i_r], full.at[i_r], partner)

    def near_got(kind, full):
        for h, d in enumerate(NEAR):
            i_r = Z * a + rem(z + Z - d)
            got(kind, i_r, full.at[i_r])
            pass_on(kind, full, i_r, d)
            send(kind + 'h', h, h, half(full.at[i_r], h), half(full.at[i_r], h), col(d))

    def far_got(kind, full):
        i_r = Z * a + rem(z + 2)
        for h in range(2):
            got(kind + 'h', h, half(full.at[i_r], h))
        pass_on(kind, full, i_r, 2)

    def passed(kind, full, d):
        i_r = Z * pa + rem(z + Z - d)
        if d:
            got(kind + 'f', rem(i_r), full.at[i_r])
        else:
            got(kind, i_r, full.at[i_r])

    kv_share()
    when(a == 1, near_send, 'q', q_all)
    dqt[...] = jnp.zeros(dqt.shape, f32)
    ot[...] = jnp.zeros(ot.shape, f32)
    m_run[...] = jnp.full(m_run.shape, NEG, f32)
    l_run[...] = jnp.zeros(l_run.shape, f32)
    kv_spread()

    @pl.when(a == 1)
    def _():
        near_got('q', q_all)
        near_send('do', do_all)
    when(a == 0, near_send, 'q', q_all)

    def full_count(i):
        n = jnp.int32(0)
        for s in QUAD:
            n = n + (g_of(s) < i).astype(i32)
        return n

    def cache_at(i, s):
        n = i - g_of(s) - 1
        for r in OFFS:
            n = n + (r <= s) * (LAST - g_of(r - 1))
        return n

    def seen(j, ct):
        key_id = j * T + lax.broadcasted_iota(i32, (T, T), 0)
        pos = (ct * T + lax.broadcasted_iota(i32, (1, T), 1)) // Z
        last = SUB * m_blk + jnp.clip(pos - SUB * z, -1, SUB - 1)
        return key_id <= last

    def fold(p):
        return p.reshape(p.shape[0] // 8, 8, p.shape[1])

    def fwd_scores(i, s, pc, ct, j, mx, masked=False):
        t = dot(k_all[s, tile(j), :], q_all[i, tile(ct), :], 1, 1) * SCALE2
        if masked:
            t = jnp.where(seen(j, ct), t, -jnp.inf)
        cache[pc, tile(j), tile(ct)] = t
        r = jnp.max(fold(t), axis=0)
        return r if mx is None else jnp.maximum(mx, r)

    def fwd_first(i, s, pc, masked=False):
        mx = None
        for j in TILES:
            mx = fwd_scores(i, s, pc, 0, j, mx, masked)
        return mx

    def fwd_pair(i, s, pc, mx, i_n, pc_n, masked=False):
        for ct in TILES:
            cs = tile(ct)
            last = ct == NT - 1
            nxt = (i_n, s, pc_n, 0) if last else (i, s, pc, ct + 1)
            m_old = m_run[i, :, cs]
            m_new = jnp.maximum(m_old, jnp.max(mx, axis=0, keepdims=True))
            al = jnp.exp2(m_old - m_new)
            mx = None
            lp = None
            o = None
            for j in TILES:
                mx = fwd_scores(*nxt, j, mx, masked and not last)
                p = jnp.exp2(cache[pc, tile(j), cs] - m_new)
                r = jnp.sum(fold(p), axis=0)
                lp = r if lp is None else lp + r
                oj = dot(vt[s, :, tile(j)], p.astype(bf16), 1, 0)
                o = oj if o is None else o + oj
            l_run[i, :, cs] = l_run[i, :, cs] * al + jnp.sum(lp, axis=0, keepdims=True)
            ot[i, :, cs] = ot[i, :, cs] * al + o
            m_run[i, :, cs] = m_new
        return mx

    def spread(lo, k):
        return lo + rem(z + k + (k >= 2) * (5 - 2 * k))

    def fwd_seg(e):
        s = rem(e)
        g = g_of(s)
        hi = jnp.where(e < Z, G, Z)

        def plain():
            @pl.when(e == 0)
            def _():
                @pl.when(a == 0)
                def _():
                    passed('q', q_all, 0)
                    for d in NEAR:
                        passed('q', q_all, d)

            def pair(k, mx):
                when((e == 0) & (k == 1) & (a == 1), far_got, 'q', q_all)
                when((e == 0) & (k == 2) & (a == 0), passed, 'q', q_all, 2)
                i = spread(Z, k)
                i_n = spread(Z, jnp.minimum(k + 1, Z - 1))
                return fwd_pair(i, s, cache_at(i, s), mx, i_n, cache_at(i_n, s))
            lax.fori_loop(0, Z, pair, fwd_first(spread(Z, 0), s, cache_at(spread(Z, 0), s)))

        def diagonal():
            i1 = jnp.minimum(g + 1, hi - 1)
            pc1 = jnp.where(g + 1 < hi, cache_at(i1, s), N_FULL)
            mx = fwd_pair(g, s, N_FULL, fwd_first(g, s, N_FULL, True), i1, pc1, True)

            def pair(i, mx):
                i_n = jnp.minimum(i + 1, hi - 1)
                return fwd_pair(i, s, cache_at(i, s), mx, i_n, cache_at(i_n, s))
            lax.fori_loop(g + 1, hi, pair, mx)
        when(e < Z, kv_ready, s)
        when(e < 2, plain)
        when(e >= 2, diagonal)

    def put(ref, at, *rows):
        for n, r in enumerate(rows):
            ref[(*at, slice(n, n + 1), slice(None))] = r

    def get(ref, *at):
        return [ref[(*at, slice(n, n + 1), slice(None))] for n in range(ref.shape[-2])]

    def fwd_done(i, c):
        z_i = rem(i)
        d_part = jnp.sum(do_all[i].T.astype(f32) * ot[i], axis=0, keepdims=True)
        put(st_loc, (i,), m_run[i], l_run[i], d_part)

        @pl.when(div(i) != a)
        def _():
            send('st', z_i, z_i, st_loc.at[i], st_par.at[z_i], partner)
        return c

    def out_give():
        for n in QUAD:
            send('o', n, n, ot.at[Z * pa + n], or1.at[n], partner)

    def pair_done(z_o):
        i = Z * a + z_o
        got('st', z_o, st_par.at[z_o])
        mine = get(st_loc, i)
        other = get(st_par, z_o)
        top = jnp.maximum(mine[0], other[0])
        w0 = jnp.exp2(mine[0] - top)
        w1 = jnp.exp2(other[0] - top)
        put(st_col, (z_o, z), top, *[w0 * p + w1 * q for p, q in zip(mine[1:], other[1:])])
        for d in OFFS:
            send('sz', Z * z_o + d, Z * z_o + d, st_col.at[z_o, z], st_col.at[z_o, z], col(d))

    def out_join(z_o):
        i = Z * a + z_o
        got('o', z_o, or1.at[z_o])
        top = get(st_col, z_o, z)[0]
        w0 = jnp.exp2(get(st_loc, i)[0] - top)
        w1 = jnp.exp2(get(st_par, z_o)[0] - top)
        for ct in TILES:
            cs = tile(ct)
            ot[i, :, cs] = ot[i, :, cs] * w0[:, cs] + or1[z_o, :, cs] * w1[:, cs]
        h = rem(z_o + Z - z)

        @pl.when(h != 0)
        def _():
            send('oz', z_o, h, ot.at[i], or2.at[h - 1], dev(a, z_o, y, x))

    def col_done(z_o):
        i = Z * a + z_o
        for d in OFFS:
            got('sz', Z * z_o + d, st_col.at[z_o, rem(z + Z - d)])
        parts = [get(st_col, z_o, n) for n in QUAD]
        big = functools.reduce(jnp.maximum, [p[0] for p in parts])
        w = [jnp.exp2(p[0] - big) for p in parts]
        tot = sum(wn * p[1] for wn, p in zip(w, parts))
        dsum = sum(wn * p[2] for wn, p in zip(w, parts))
        put(ld, (i,), big + jnp.log(tot) * math.log2(math.e), dsum / tot)
        send('ld', i, i, ld.at[i], ld.at[i], partner)

    def passed_all(kind, full):
        for d in (0,) + OFFS:
            passed(kind, full, d)

    def seg_step(e, c):
        fwd_seg(e)

        @pl.when(a == 1)
        def _():
            when(e == 0, near_got, 'do', do_all)
            when(e == 1, far_got, 'do', do_all)

            @pl.when(e == 1)
            def _():
                for d in (0,) + NEAR:
                    passed('q', q_all, d)

            @pl.when(e == 3)
            def _():
                passed('q', q_all, 2)
                lax.fori_loop(Z, G, fwd_done, 0)
                for n in (3, 2, 1, 0):
                    pair_done(n)

            @pl.when(e == 4)
            def _():
                for n in (3, 2, 1, 0):
                    col_done(n)

            @pl.when(e == 5)
            def _():
                passed_all('do', do_all)
                lax.fori_loop(0, Z, fwd_done, 0)
                out_give()
                for d in (2, 1, 3, 0):
                    out_join(rem(z + d))

        @pl.when(a == 0)
        def _():
            @pl.when(e == 0)
            def _():
                near_got('q', q_all)
                near_send('do', do_all)
            when(e == 1, far_got, 'q', q_all)
            when(e == 2, near_got, 'do', do_all)

            @pl.when(e == 3)
            def _():
                passed_all('do', do_all)
                lax.fori_loop(Z, G, fwd_done, 0)
                out_give()
                far_got('do', do_all)

            @pl.when(e == 5)
            def _():
                lax.fori_loop(0, Z, fwd_done, 0)
        return c
    lax.fori_loop(0, 6, seg_step, 0)

    def dq_join(z_o):
        i = Z * a + z_o
        got('g', z_o, dqr1.at[z_o])
        for ct in TILES:
            cs = tile(ct)
            dqt[i, :, cs] = dqt[i, :, cs] + dqr1[z_o, :, cs]
        h = rem(z_o + Z - z)

        @pl.when(h != 0)
        def _():
            send('gz', z_o, h, dqt.at[i], dqr2.at[h - 1], dev(a, z_o, y, x))

    def bwd_scores(i, s, u, masked):
        j, ct = divmod(u, NT)
        dpb[u % NT] = dot(v_all[s, tile(j), :], do_all[i, tile(ct), :], 1, 1)
        if masked:
            t = dot(k_all[s, tile(j), :], q_all[i, tile(ct), :], 1, 1) * SCALE2
            scb[u % NT] = jnp.where(seen(j, ct), t, -jnp.inf)

    def bwd_pair(i, s, pc, s_n, masked=False):
        acc_v = None
        acc_k = None
        pend = None

        def products(u, p, ds, acc_v, acc_k):
            j, ct = divmod(u, NT)
            e = dot(p, do_all[i, tile(ct), :], 1, 0)
            g = dot(ds, q_all[i, tile(ct), :], 1, 0)
            acc_v = e if ct == 0 else acc_v + e
            acc_k = g if ct == 0 else acc_k + g
            dqt[i, :, tile(ct)] += dot(kt[s, :, tile(j)], ds, 1, 0)
            if ct == NT - 1:
                dv[s, tile(j), :] += acc_v
                dk[s, tile(j), :] += acc_k
            return acc_v, acc_k

        n_u = NT * NT
        for u in range(n_u):
            j, ct = divmod(u, NT)
            if u < n_u - 1:
                bwd_scores(i, s, u + 1, masked)
            else:
                bwd_scores(i, s_n, 0, False)
            t = scb[u % NT] if masked else cache[pc, tile(j), tile(ct)]
            p = jnp.exp2(t - ld[i, 0:1, tile(ct)])
            ds = p * (dpb[u % NT] - ld[i, 1:2, tile(ct)])
            now = p.astype(bf16), ds.astype(bf16)
            if pend is not None:
                acc_v, acc_k = products(u - 1, *pend, acc_v, acc_k)
            pend = now
        products(n_u - 1, *pend, acc_v, acc_k)

    def bwd_block(i, lo, hi):
        end = jnp.minimum(full_count(i), hi)
        s_d = 2 * div(i) + div(rem(i), 2)
        diag = (rem(div(i) + i, 2) == a) & (s_d >= lo) & (s_d < hi)

        @pl.when(diag)
        def _():
            bwd_scores(i, s_d, 0, True)
            bwd_pair(i, s_d, N_FULL, lo, True)

        @pl.when(jnp.logical_not(diag) & (lo < end))
        def _():
            bwd_scores(i, lo, 0, False)

        def pair(s, c):
            bwd_pair(i, s, cache_at(i, s), jnp.minimum(s + 1, Z - 1))
            return c
        lax.fori_loop(lo, end, pair, 0)

    dk5 = dk.reshape(Z, Z, Z, SUB, HD)
    dv5 = dv.reshape(Z, Z, Z, SUB, HD)
    dkr14 = dkr1.reshape(Z, 3, Z, SUB, HD)
    dvr14 = dvr1.reshape(Z, 3, Z, SUB, HD)
    dk24 = dk2.reshape(Z, Z, SUB, HD)
    dv24 = dv2.reshape(Z, Z, SUB, HD)

    def kv_first(s):
        for d in OFFS:
            n = Z * s + d
            send('rk', n, n, dk5.at[s, rem(y + d)], dkr14.at[s, d - 1], in_y(d))
            send('rv', n, n, dv5.at[s, :, rem(x + d)], dvr14.at[s, d - 1], in_x(d))

    def kv_second(s):
        for d in OFFS:
            got('rk', Z * s + d, dkr14.at[s, d - 1])
            got('rv', Z * s + d, dvr14.at[s, d - 1])
        dk2[s] = dk[s, pl.ds(pl.multiple_of(BLK * y, BLK), BLK), :] + sum(dkr1[s, d - 1] for d in OFFS)
        for n in QUAD:
            rows = slice(n * SUB, (n + 1) * SUB)
            dv2[s, rows, :] = dv[s, sub_rows(Z * n + x), :] + sum(dvr1[s, d - 1, rows, :] for d in OFFS)
        for d in OFFS:
            n = Z * s + d
            send('sk', n, n, dk24.at[s, rem(x + d)], dkr2.at[s, d - 1], in_x(d))
            send('sv', n, n, dv24.at[s, rem(y + d)], dvr2.at[s, d - 1], in_y(d))

    def kv_third(s):
        for d in OFFS:
            got('sk', Z * s + d, dkr2.at[s, d - 1])
            got('sv', Z * s + d, dvr2.at[s, d - 1])
        kst[s] = ((dk2[s, sub_rows(x), :] + sum(dkr2[s, d - 1] for d in OFFS)) * SCALE).astype(bf16)
        vst[s] = (dv2[s, sub_rows(y), :] + sum(dvr2[s, d - 1] for d in OFFS)).astype(bf16)
        a_s, z_s = group_of(s)
        rows = sub_rows(z)

        @pl.when(g_of(s) == i_own)
        def _():
            dk_fin[rows, :] = kst[s]
            dv_fin[rows, :] = vst[s]

        @pl.when(not_mine(s))
        def _():
            to = dev(a_s, z_s, y, x)
            send('fk', s, rem(z_s + Z - z), kst.at[s], dk_fin.at[rows], to)
            send('fv', s, rem(z_s + Z - z), vst.at[s], dv_fin.at[rows], to)

    def rot(k):
        return rem(z + 2 + Z - k + 3 * (k == 2) + (k == 3))

    def bwd_step(n, c):
        mid = (n == 4) | (n == 5)
        late = n >= 6
        i = jnp.where(mid, n - 2, jnp.where(late, rot(n - 6), LAST - n))
        lo = mid.astype(i32)
        hi = jnp.where(mid, 2, jnp.where(late, 1, Z))
        a_i = div(i)
        z_i = rem(i)
        when((a_i != a) & ((n < 6) | (z_i < 2)), got, 'ld', i, ld.at[i])
        bwd_block(i, lo, hi)

        @pl.when((a_i != a) & jnp.logical_not(mid))
        def _():
            send('g', z_i, z_i, dqt.at[i], dqr1.at[z_i], partner)
        for s in QUAD:
            when(n == (9, 5, 2, 0)[s] + a * (0, 0, 1, 1)[s], kv_first, s)

        @pl.when(a == 0)
        def _():
            @pl.when(n == 0)
            def _():
                for k in (2, 3, 1, 0):
                    pair_done(k)
                for d in (2, 1, 3, 0):
                    out_join(rem(z + d))

            @pl.when(n == 2)
            def _():
                for k in (2, 3, 1, 0):
                    col_done(k)
            when(n >= 7, dq_join, rot(n - 7))
        when((a == 1) & (n >= 1) & (n <= 4), dq_join, 4 - n)
        when(n == 2 + a, kv_second, 3)
        when(n == 5 + 2 * a, kv_second, 2)
        when(n == 6, kv_third, 3)
        when(n == 9, kv_third, 2)
        return c
    lax.fori_loop(0, 10, bwd_step, 0)

    when(a == 0, dq_join, z)
    kv_second(1)
    for h in OFFS:
        got('oz', h, or2.at[h - 1])
    w_z = [jnp.exp2(get(st_col, z, rem(z + Z - h))[0] - ld[i_own, 0:1, :]) for h in QUAD]
    for ct in TILES:
        cs = tile(ct)
        o = ot[i_own, :, cs] * w_z[0][:, cs]
        for h in OFFS:
            o = o + or2[h - 1, :, cs] * w_z[h][:, cs]
        o_out[cs, :] = o.T.astype(bf16)
    kv_second(0)
    kv_third(1)
    kv_third(0)
    for h in OFFS:
        got('gz', h, dqr2.at[h - 1])
    for ct in TILES:
        cs = tile(ct)
        dq_out[cs, :] = ((dqt[i_own, :, cs] + sum(dqr2[h - 1, :, cs] for h in OFFS)).T * SCALE).astype(bf16)
    for h in QUAD:
        rows = sub_rows(rem(z + Z - h))

        def take():
            got('fk', h, dk_fin.at[rows])
            got('fv', h, dv_fin.at[rows])
        if h:
            take()
        else:
            when(jnp.logical_not(keep), take)
    dk_out[...] = dk_fin[...]
    dv_out[...] = dv_fin[...]

    def left(n):
        sent('ka', n, k_loc.at[pl.ds(0, SUB)])
        sent('va', n, v_loc.at[pl.ds(0, SUB)])
    when(jnp.logical_not(keep), left, 0)
    for kind, full in (('q', q_all), ('do', do_all)):
        sent(kind, i_own, full.at[i_own])
        for h, d in enumerate(NEAR):
            sent(kind, rem(i_own + d, G), full.at[i_own])
            sent(kind + 'h', h, half(full.at[i_own], h))
        for d in OFFS:
            sent(kind + 'f', d, full.at[i_own])
    for d in OFFS:
        left(d)
        sent('kx', d, k5.at[:, y, x])
        sent('vy', d, v5.at[:, y, x])
    for s in QUAD:
        sent('st', s, st_par.at[s])
        sent('o', s, or1.at[s])
        sent('g', s, or1.at[s])
        sent('ld', Z * a + s, ld.at[s])

        @pl.when(s != z)
        def _():
            sent('oz', s, or1.at[s])
            sent('gz', s, or1.at[s])

        @pl.when(not_mine(s))
        def _():
            sent('fk', s, kst.at[s])
            sent('fv', s, vst.at[s])
        for d in OFFS:
            n = Z * s + d
            sent('sz', n, st_col.at[s, 0])
            sent('ky', n, k5.at[s, y])
            sent('vx', n, v5.at[s, :, x])
            sent('rk', n, dkr14.at[s, 0])
            sent('rv', n, dvr14.at[s, 0])
            sent('sk', n, dkr2.at[s, 0])
            sent('sv', n, dvr2.at[s, 0])


def solution(mesh):
    blk_spec = P('data', CTX_AXES, None, None)
    v = pltpu.VMEM
    big = (ROWS, HD)
    big_t = (HD, ROWS)
    blk = (BLK, HD)
    sub = (SUB, HD)
    scratch = [
        *[v(blk, bf16)] * 2,
        *[v((G,) + big, bf16)] * 2, *[v((Z,) + big, bf16)] * 2,
        *[v((Z,) + big_t, bf16)] * 2,
        *[v((G,) + big_t, f32)] * 2, *[v((Z,) + big, f32)] * 2,
        v((N_FULL + 1, ROWS, ROWS), f32),
        *[v((NT, T, T), f32)] * 2, v((8, T), f32),
        *[v((G, 1, ROWS), f32)] * 2, v((G, 3, ROWS), f32),
        v((Z, 3, ROWS), f32), v((Z, Z, 3, ROWS), f32), v((G, 2, ROWS), f32),
        *[v((Z,) + big_t, f32), v((3,) + big_t, f32)] * 2,
        *[v((Z, 3) + blk, f32)] * 2, *[v((Z,) + blk, f32)] * 2,
        *[v((Z, 3) + sub, f32)] * 2, *[v((Z,) + sub, bf16)] * 2,
        *[v(blk, bf16)] * 2,
        *[pltpu.SemaphoreType.DMA((N_SEM,))] * 2,
    ]
    call = pl.pallas_call(
        body,
        name='attn',
        out_shape=[jax.ShapeDtypeStruct(big, bf16)] * 2 + [jax.ShapeDtypeStruct(blk, bf16)] * 2,
        in_specs=[pl.BlockSpec(memory_space=pl.ANY)] * 4,
        out_specs=[pl.BlockSpec(memory_space=pltpu.VMEM)] * 4,
        scratch_shapes=scratch,
        compiler_params=pltpu.CompilerParams(collective_id=0, has_side_effects=True, vmem_limit_bytes=67043328),
    )

    def hand_out(*refs):
        for src, dst in zip(refs[:Z], refs[Z:]):
            dst[...] = src[...]

    leave = pl.pallas_call(
        hand_out,
        name='leave',
        out_shape=[jax.ShapeDtypeStruct(big, bf16)] * 2 + [jax.ShapeDtypeStruct(blk, bf16)] * 2,
        in_specs=[pl.BlockSpec(memory_space=pltpu.VMEM)] * 4,
        out_specs=[pl.BlockSpec(memory_space=pltpu.VMEM)] * 4,
    )

    def local_attn(q_in, k_in, v_in, do_in):
        o, dq, dk, dv = leave(*call(q_in.reshape(big), k_in.reshape(blk), v_in.reshape(blk), do_in.reshape(big)))
        return o.reshape(q_in.shape), dq.reshape(q_in.shape), dk.reshape(k_in.shape), dv.reshape(k_in.shape)

    return jax.shard_map(local_attn, mesh=mesh, in_specs=(blk_spec,) * 4, out_specs=(blk_spec,) * 4, check_vma=False)
```

time: 3680 us -> 95.1 us (0.03)
  waiting for transfers between devices: 2930 us -> 0 us
  starting transfers between devices: 421 us -> 0 us
  matrix products: 160 us -> 0 us
  local copies, waits for them, and re-layouts: 132 us -> 0 us
  Pallas kernels: 0 us -> 94.3 us
    ppermute x893 -> x0, waiting for transfers between devices: 2930 us -> none  [the longest x888 2910 us: send_next(): return lax.ppermute(tree_in, CTX_AXES, next_perm)]
    ppermute x893 -> x0, starting transfers between devices: 421 us -> none  [the longest x888 420 us: send_next(): return lax.ppermute(tree_in, CTX_AXES, next_perm)]
    dot_general x454 -> x0, matrix products: 160 us -> none  [the longest x65 38.1 us: pair_forward(): jnp.einsum('bhqgk,bkhd->bhqgd', prob_blk.astype(jnp.bfloat16), v_blk, pre...]
    while x693 -> x0, local copies, waits for them, and re-layouts: 124 us -> none
    pallas_call x0 -> x2, Pallas kernels: none -> 94.3 us  [the longest x1 92.5 us: local_attn(): call(q_in.reshape(big), k_in.reshape(blk), v_in.reshape(blk), do_in.resha...]
  transfers between devices with their start and end apart: 893 -> 0, of which waited for: 400 -> 0; matrix products, arithmetic and copies ran while one was open for 6% -> 0% of each run, Pallas kernels for 0% -> 0%
where the time goes in v3:
time: 95.1 us; the launch traced here: 95 us
  Pallas kernels  94.3 us (99%)
    pallas_call x1, Pallas kernels, local_attn(): call(q_in.reshape(big), k_in.reshape(blk), v_in.reshape(blk), do_in.resha...  92.5 us

profile of v3, /device:TPU:0, one launch (start us, length us, event | category | flops | bytes accessed | tf_op | source)
XLA Modules:
  0.0 95.0 jit_solution(14329930616985701889)
XLA Ops:
  0.6 92.5 %attn.1 = (bf16[768,128]{1,0:T(8,128)(2,1)}, bf16[768,128]{1,0:T(8,128)(2,1)}, bf16[192,128]{1,0:T(8,128)(2,1)}, bf16[192,128]{1,0:T(8,128)(2,1)}) custom-call(bf16[768,128]{1,0:T(8,128)(2,1)} %bitcast.8, bf16[192,128]{1,0:T(8,128)(2,1)} %bitcast.10, bf16[192,128]{1,0:T(8,128)(2,1)} %bitcast.11, bf16[768,128]{1,0:T(8,128)(2,1)} %bitcast.9), custom_call_target="tpu_custom_call" | custom-call | tf_op jit(solution)/shard_map/attn/pallas_call | solution.py:725
  93.1 1.8 %leave.1 = (bf16[768,128]{1,0:T(8,128)(2,1)}, bf16[768,128]{1,0:T(8,128)(2,1)}, bf16[192,128]{1,0:T(8,128)(2,1)}, bf16[192,128]{1,0:T(8,128)(2,1)}) custom-call(bf16[768,128]{1,0:T(8,128)(2,1)} %get-tuple-element.12.refs_0_, bf16[768,128]{1,0:T(8,128)(2,1)} %get-tuple-element.13.refs_1_, bf16[192,128]{1,0:T(8,128)(2,1)} %get-tuple-element.14.refs_2_, ...), custom_call_target="tpu_custom_call" | custom-call | tf_op jit(solution)/shard_map/leave/pallas_call | solution.py:725

commit v4 on v3

v4 whole, which is shorter than its diff:
```python
import functools
import math
import jax
import jax.numpy as jnp
from jax import lax
from jax.experimental import pallas as pl
from jax.experimental.pallas import tpu as pltpu
from jax.sharding import PartitionSpec as P

CTX_AXES = ('ctxo', 'ctx')
MESH = pl.DeviceIdType.MESH
f32 = jnp.float32
bf16 = jnp.bfloat16
i32 = jnp.int32

Z = 4
G = 8
HD = 128
SUB = 48
BLK = Z * SUB
ROWS = Z * BLK
HALF = ROWS // 2
T = 256
NT = ROWS // T
TILES = range(NT)
QUAD = range(Z)
OFFS = (1, 2, 3)
NEAR = (1, 3)
SCALE = 1.0 / math.sqrt(HD)
SCALE2 = SCALE * math.log2(math.e)
NEG = -1e30
N_PAIR = 18
LAST = G - 1

KINDS = {'ka': Z, 'va': Z, 'kx': 1, 'vy': 1, 'ky': Z, 'vx': Z,
         'q': 3, 'qh': 2, 'qf': Z, 'do': 3, 'doh': 2, 'dof': Z,
         'st': Z, 'sz': Z, 'ld': Z, 'o': Z, 'oz': 1, 'g': Z, 'gz': 1,
         'rk': Z, 'rv': Z, 'sk': Z, 'sv': Z, 'fk': 2, 'fv': 2}
N_RECV = sum(KINDS.values())
N_SEND = len(KINDS) + 2 * Z


def dot(a, b, ca, cb):
    return lax.dot_general(a, b, (((ca,), (cb,)), ((), ())), preferred_element_type=f32)


def tile(n):
    return slice(n * T, (n + 1) * T)


def rem(n, k=Z):
    return n % k if isinstance(n, int) else lax.rem(n, jnp.int32(k))


def div(n, k=Z):
    return n // k if isinstance(n, int) else lax.div(n, jnp.int32(k))


def sub_rows(n):
    return pl.ds(pl.multiple_of(SUB * n, SUB), SUB)


def body(q_hbm, k_hbm, v_hbm, do_hbm, o_hbm, dq_hbm, dk_hbm, dv_hbm,
         k_loc, v_loc, q_all, do_all, k_all, v_all, kt, vt, acc, dk, dv, cache, dpb,
         m_run, l_run, st_loc, st_par, st_col, ld,
         or1, or2, dqr2, dkr1, dvr1, dkr2, dvr2, kst, vst, dk_fin, dv_fin, s_sem, r_sem, room):
    a = lax.axis_index('ctxo')
    b = lax.axis_index('ctx')
    z = div(b, Z * Z)
    y = rem(div(b))
    x = rem(b)
    m_blk = Z * y + x
    i_own = Z * a + z
    pa = 1 - a
    par = rem(a + z, 2)
    names = list(KINDS)
    base = {kind: sum(KINDS[k] for k in names[:n]) for n, kind in enumerate(names)}

    def dev(a_, z_, y_, x_):
        return {'ctxo': a_, 'ctx': Z * Z * z_ + Z * y_ + x_}

    partner = dev(pa, z, y, x)

    def col(d):
        return dev(a, rem(z + d), y, x)

    def other_col(d):
        return dev(pa, rem(z + d), y, x)

    def in_y(d):
        return dev(a, z, rem(y + d), x)

    def in_x(d):
        return dev(a, z, y, rem(x + d))

    def rc(kind, n, src, dst, to):
        return pltpu.make_async_remote_copy(src_ref=src, dst_ref=dst, send_sem=s_sem.at[names.index(kind)], recv_sem=r_sem.at[base[kind] + n],
                                            device_id=to, device_id_type=MESH)

    def send(kind, n, src, dst, to):
        rc(kind, n, src, dst, to).start()

    def got(kind, n, ref):
        rc(kind, n, ref, ref, partner).wait_recv()

    def sent(kind, ref):
        rc(kind, 0, ref, ref, partner).wait_send()

    def when(cond, fn, *args):
        pl.when(cond)(functools.partial(fn, *args))

    def group_of(s):
        a_s = div(s, 2)
        return a_s, 2 * rem(s, 2) + rem(a_s + a, 2)

    def g_of(s):
        a_s, z_s = group_of(s)
        return Z * a_s + z_s

    def not_mine(s):
        return g_of(s) != i_own

    own = [(q_hbm, q_all.at[i_own]), (do_hbm, do_all.at[i_own]), (k_hbm, k_loc), (v_hbm, v_loc)]
    own = [pltpu.make_async_copy(src, dst, s_sem.at[len(KINDS) + n]) for n, (src, dst) in enumerate(own)]
    for c in reversed(own):
        c.start()
    bar = pltpu.get_barrier_semaphore()
    peers = [partner] + [f(d) for d in OFFS for f in (col, other_col, in_y, in_x)]
    for to in peers:
        pl.semaphore_signal(bar, inc=1, device_id=to, device_id_type=MESH)
    for c in reversed(own):
        c.wait()
    pl.semaphore_wait(bar, len(peers))

    QUADS = pl.ds(0, Z)
    OTHERS = pl.ds(0, 3)
    k5 = k_all.reshape(Z, Z, Z, SUB, HD)
    v5 = v_all.reshape(Z, Z, Z, SUB, HD)

    s_me = 2 * a + div(z, 2)
    keep = par == a
    for d in QUAD:
        rows = sub_rows(rem(z + d))
        to = dev(par, rem(z + d), y, x)

        def give():
            send('ka', s_me, k_loc.at[rows], k5.at[s_me, y, x], to)
            send('va', s_me, v_loc.at[rows], v5.at[s_me, y, x], to)

        if d:
            give()
        else:
            @pl.when(keep)
            def _():
                k_all[s_me, sub_rows(m_blk), :] = k_loc[rows, :]
                v_all[s_me, sub_rows(m_blk), :] = v_loc[rows, :]
            when(jnp.logical_not(keep), give)
    send('q', 2, q_all.at[i_own], q_all.at[i_own], partner)
    send('do', 2, do_all.at[i_own], do_all.at[i_own], partner)
    dk[...] = jnp.zeros(dk.shape, f32)
    dv[...] = jnp.zeros(dv.shape, f32)

    def kv_share():
        for s in QUAD:
            @pl.when(not_mine(s))
            def _():
                got('ka', s, k5.at[s, y, x])
                got('va', s, v5.at[s, y, x])
        for d in OFFS:
            send('kx', 0, k5.at[:, y, x], k5.at[:, y, x], in_x(d))
            send('vy', 0, v5.at[:, y, x], v5.at[:, y, x], in_y(d))

    def kv_spread():
        got('kx', 0, k5.at[:, OTHERS, 0])
        got('vy', 0, v5.at[:, OTHERS, 0])
        for s in QUAD:
            for d in OFFS:
                send('ky', s, k5.at[s, y], k5.at[s, y], in_y(d))
                send('vx', s, v5.at[s, :, x], v5.at[s, :, x], in_x(d))

    def kv_ready(s):
        got('ky', s, k5.at[s, OTHERS])
        got('vx', s, v5.at[s, OTHERS])
        kt[s] = k_all[s].T
        vt[s] = v_all[s].T

    def half(ref, h):
        return ref.at[pl.ds(h * HALF, HALF)]

    def near_send(kind, full):
        for h, d in enumerate(NEAR):
            send(kind, h, full.at[i_own], full.at[i_own], col(d))

    def pass_on(kind, full, i_r, n):
        send(kind + 'f', n, full.at[i_r], full.at[i_r], partner)

    def near_got(kind, full):
        for h, d in enumerate(NEAR):
            i_r = Z * a + rem(z + Z - d)
            got(kind, h, full.at[i_r])
            pass_on(kind, full, i_r, d)
            send(kind + 'h', h, half(full.at[i_r], h), half(full.at[i_r], h), col(d))

    def far_got(kind, full):
        i_r = Z * a + rem(z + 2)
        for h in range(2):
            got(kind + 'h', h, half(full.at[i_r], h))
        pass_on(kind, full, i_r, 2)

    def passed(kind, full, d):
        i_r = Z * pa + rem(z + Z - d)
        if d:
            got(kind + 'f', d, full.at[i_r])
        else:
            got(kind, 2, full.at[i_r])

    kv_share()
    when(a == 1, near_send, 'q', q_all)
    acc[...] = jnp.zeros(acc.shape, f32)
    m_run[...] = jnp.full(m_run.shape, NEG, f32)
    l_run[...] = jnp.zeros(l_run.shape, f32)
    kv_spread()

    @pl.when(a == 1)
    def _():
        near_got('q', q_all)
        near_send('do', do_all)
    when(a == 0, near_send, 'q', q_all)

    def cache_at(i, s):
        n = i - g_of(s)
        for r in OFFS:
            n = n + (r <= s) * (G - g_of(r - 1))
        return n

    def dq_at(i):
        return jnp.where(div(i) == a, G + rem(i), i)

    def seen(j, ct):
        key_id = j * T + lax.broadcasted_iota(i32, (T, T), 0)
        pos = (ct * T + lax.broadcasted_iota(i32, (1, T), 1)) // Z
        last = SUB * m_blk + jnp.clip(pos - SUB * z, -1, SUB - 1)
        return key_id <= last

    def fold(p):
        return p.reshape(p.shape[0] // 8, 8, p.shape[1])

    def fwd_scores(i, s, pc, ct, j, mx, masked=False):
        t = dot(k_all[s, tile(j), :], q_all[i, tile(ct), :], 1, 1) * SCALE2
        if masked:
            t = jnp.where(seen(j, ct), t, -jnp.inf)
        cache[pc, tile(j), tile(ct)] = t
        r = jnp.max(fold(t), axis=0)
        return r if mx is None else jnp.maximum(mx, r)

    def fwd_first(i, s, masked=False):
        mx = None
        for j in TILES:
            mx = fwd_scores(i, s, cache_at(i, s), 0, j, mx, masked)
        return mx

    def fwd_pair(i, s, mx, i_n, s_n, pc, pc_n, masked=False):
        for ct in TILES:
            cs = tile(ct)
            last = ct == NT - 1
            nxt = (i_n, s_n, pc_n, 0) if last else (i, s, pc, ct + 1)
            m_old = m_run[i, :, cs]
            m_new = jnp.maximum(m_old, jnp.max(mx, axis=0, keepdims=True))
            al = jnp.exp2(m_old - m_new)
            mx = None
            lp = None
            o = None
            for j in TILES:
                mx = fwd_scores(*nxt, j, mx, masked and not last)
                p = jnp.exp2(cache[pc, tile(j), cs] - m_new)
                r = jnp.sum(fold(p), axis=0)
                lp = r if lp is None else lp + r
                oj = dot(vt[s, :, tile(j)], p.astype(bf16), 1, 0)
                o = oj if o is None else o + oj
            l_run[i, :, cs] = l_run[i, :, cs] * al + jnp.sum(lp, axis=0, keepdims=True)
            acc[i, :, cs] = acc[i, :, cs] * al + o
            m_run[i, :, cs] = m_new
        return mx

    def spread(lo, k):
        return lo + rem(z + k + (k >= 2) * (5 - 2 * k))

    def fwd_seg(e):
        s = rem(e)
        g = g_of(s)
        hi = jnp.where(e < Z, G, Z)
        at = cache_at(0, s)

        def plain():
            @pl.when(e == 0)
            def _():
                @pl.when(a == 0)
                def _():
                    passed('q', q_all, 0)
                    for d in NEAR:
                        passed('q', q_all, d)

            def pair(k, mx):
                when((e == 0) & (k == 1) & (a == 1), far_got, 'q', q_all)
                when((e == 0) & (k == 2) & (a == 0), passed, 'q', q_all, 2)
                i = spread(Z, k)
                i_n = spread(Z, jnp.minimum(k + 1, Z - 1))
                return fwd_pair(i, s, mx, i_n, s, at + i, at + i_n)
            lax.fori_loop(0, Z, pair, fwd_first(spread(Z, 0), s))

        def diagonal():
            more = g + 1 < hi
            mx = fwd_pair(g, s, fwd_first(g, s, True), jnp.where(more, g + 1, LAST), jnp.where(more, s, 0),
                          at + g, jnp.where(more, at + g + 1, cache_at(LAST, 0)), True)

            def pair(i, mx):
                i_n = jnp.minimum(i + 1, hi - 1)
                return fwd_pair(i, s, mx, i_n, s, at + i, at + i_n)
            lax.fori_loop(g + 1, hi, pair, mx)
        when(e < Z, kv_ready, s)
        when(e < 2, plain)
        when(e >= 2, diagonal)

    def put(ref, at, *rows):
        for n, r in enumerate(rows):
            ref[(*at, slice(n, n + 1), slice(None))] = r

    def get(ref, *at):
        return [ref[(*at, slice(n, n + 1), slice(None))] for n in range(ref.shape[-2])]

    def fwd_done(i, c):
        z_i = rem(i)
        d_part = jnp.sum(do_all[i].T.astype(f32) * acc[i], axis=0, keepdims=True)
        put(st_loc, (i,), m_run[i], l_run[i], d_part)

        @pl.when(div(i) != a)
        def _():
            send('st', z_i, st_loc.at[i], st_par.at[z_i], partner)
        return c

    def out_give():
        for n in QUAD:
            send('o', n, acc.at[Z * pa + n], or1.at[n], partner)

    def pair_done(z_o):
        i = Z * a + z_o
        got('st', z_o, st_par.at[z_o])
        mine = get(st_loc, i)
        other = get(st_par, z_o)
        top = jnp.maximum(mine[0], other[0])
        w0 = jnp.exp2(mine[0] - top)
        w1 = jnp.exp2(other[0] - top)
        put(st_col, (z_o, z), top, *[w0 * p + w1 * q for p, q in zip(mine[1:], other[1:])])
        for d in OFFS:
            send('sz', z_o, st_col.at[z_o, z], st_col.at[z_o, z], col(d))

    def out_join(z_o):
        i = Z * a + z_o
        got('o', z_o, or1.at[z_o])
        top = get(st_col, z_o, z)[0]
        w0 = jnp.exp2(get(st_loc, i)[0] - top)
        w1 = jnp.exp2(get(st_par, z_o)[0] - top)
        for ct in TILES:
            cs = tile(ct)
            acc[i, :, cs] = acc[i, :, cs] * w0[:, cs] + or1[z_o, :, cs] * w1[:, cs]
        h = rem(z_o + Z - z)

        @pl.when(h != 0)
        def _():
            send('oz', 0, acc.at[i], or2.at[h - 1], dev(a, z_o, y, x))

    def joins():
        for d in (2, 1, 3, 0):
            out_join(rem(z + d))
        pl.semaphore_signal(room, inc=1, device_id=partner, device_id_type=MESH)

    def col_done(z_o):
        i = Z * a + z_o
        got('sz', z_o, st_col.at[z_o, OTHERS])
        parts = [get(st_col, z_o, n) for n in QUAD]
        big = functools.reduce(jnp.maximum, [p[0] for p in parts])
        w = [jnp.exp2(p[0] - big) for p in parts]
        tot = sum(wn * p[1] for wn, p in zip(w, parts))
        dsum = sum(wn * p[2] for wn, p in zip(w, parts))
        put(ld, (i,), big + jnp.log(tot) * math.log2(math.e), dsum / tot)
        send('ld', z_o, ld.at[i], ld.at[i], partner)

    def passed_all(kind, full):
        for d in (0,) + OFFS:
            passed(kind, full, d)

    def seg_step(e, c):
        fwd_seg(e)

        @pl.when(a == 1)
        def _():
            when(e == 0, near_got, 'do', do_all)
            when(e == 1, far_got, 'do', do_all)

            @pl.when(e == 1)
            def _():
                for d in (0,) + NEAR:
                    passed('q', q_all, d)

            @pl.when(e == 3)
            def _():
                passed('q', q_all, 2)
                lax.fori_loop(Z, G, fwd_done, 0)
                for n in (3, 2, 1, 0):
                    pair_done(n)

            @pl.when(e == 4)
            def _():
                for n in (3, 2, 1, 0):
                    col_done(n)

            @pl.when(e == 5)
            def _():
                passed_all('do', do_all)
                lax.fori_loop(0, Z, fwd_done, 0)
                out_give()
                joins()

        @pl.when(a == 0)
        def _():
            @pl.when(e == 0)
            def _():
                near_got('q', q_all)
                near_send('do', do_all)
            when(e == 1, far_got, 'q', q_all)
            when(e == 2, near_got, 'do', do_all)

            @pl.when(e == 3)
            def _():
                passed_all('do', do_all)
                lax.fori_loop(Z, G, fwd_done, 0)
                out_give()
                far_got('do', do_all)

            @pl.when(e == 5)
            def _():
                lax.fori_loop(0, Z, fwd_done, 0)
        return c
    lax.fori_loop(0, 6, seg_step, 0)

    def dq_join(z_o):
        i = G + z_o
        got('g', z_o, or1.at[z_o])
        for ct in TILES:
            cs = tile(ct)
            acc[i, :, cs] = acc[i, :, cs] + or1[z_o, :, cs]
        h = rem(z_o + Z - z)

        @pl.when(h != 0)
        def _():
            send('gz', 0, acc.at[i], dqr2.at[h - 1], dev(a, z_o, y, x))

    def dq_room():
        sent('o', or1)
        for n in QUAD:
            acc[Z * pa + n] = jnp.zeros(or1.shape[1:], f32)

    def bwd_scores(i, s, u):
        j, ct = divmod(u, NT)
        dpb[u % NT] = dot(v_all[s, tile(j), :], do_all[i, tile(ct), :], 1, 1)

    def bwd_pair(i, s, i_n, s_n, pc, dq):
        acc_v = None
        acc_k = None
        pend = None

        def products(u, p, ds, acc_v, acc_k):
            j, ct = divmod(u, NT)
            e = dot(p, do_all[i, tile(ct), :], 1, 0)
            g = dot(ds, q_all[i, tile(ct), :], 1, 0)
            acc_v = e if ct == 0 else acc_v + e
            acc_k = g if ct == 0 else acc_k + g
            acc[dq, :, tile(ct)] += dot(kt[s, :, tile(j)], ds, 1, 0)
            if ct == NT - 1:
                dv[s, tile(j), :] += acc_v
                dk[s, tile(j), :] += acc_k
            return acc_v, acc_k

        n_u = NT * NT
        for u in range(n_u):
            j, ct = divmod(u, NT)
            if u < n_u - 1:
                bwd_scores(i, s, u + 1)
            else:
                bwd_scores(i_n, s_n, 0)
            p = jnp.exp2(cache[pc, tile(j), tile(ct)] - ld[i, 0:1, tile(ct)])
            ds = p * (dpb[u % NT] - ld[i, 1:2, tile(ct)])
            now = p.astype(bf16), ds.astype(bf16)
            if pend is not None:
                acc_v, acc_k = products(u - 1, *pend, acc_v, acc_k)
            pend = now
        products(n_u - 1, *pend, acc_v, acc_k)

    def rot(k):
        return rem(z + (2, 1, 3, 0)[k])

    STEPS = 10

    def bwd_part(n):
        i, lo, hi = (LAST - n, 0, Z) if n < 4 else (n - 2, 1, 2) if n < 6 else (rot(n - 6), 0, 1)
        end = jnp.int32(0)
        for s in QUAD:
            end = end + (g_of(s) <= i).astype(i32)
        return i, lo, jnp.minimum(end, hi)

    def bwd_block(n):
        i, lo, end = bwd_part(n)
        i_n, lo_n, _ = bwd_part(min(n + 1, STEPS - 1))
        _, lo_p, end_p = bwd_part(max(n - 1, 0))

        if n == 0:
            bwd_scores(i, lo, 0)
        elif n > 4:
            when((lo < end) & (lo_p >= end_p), bwd_scores, i, lo, 0)
        dq = dq_at(i)

        def pair(s, c):
            more = s + 1 < end
            bwd_pair(i, s, jnp.where(more, i, i_n), jnp.where(more, s + 1, lo_n), cache_at(i, s), dq)
            return c
        lax.fori_loop(lo, end, pair, 0)

    dk5 = dk.reshape(Z, Z, Z, SUB, HD)
    dv5 = dv.reshape(Z, Z, Z, SUB, HD)
    dkr14 = dkr1.reshape(Z, 3, Z, SUB, HD)
    dvr14 = dvr1.reshape(Z, 3, Z, SUB, HD)

    def kv_first(s):
        for d in OFFS:
            send('rk', s, dk5.at[s, rem(y + d)], dkr14.at[s, d - 1], in_y(d))
            send('rv', s, dv5.at[s, :, rem(x + d)], dvr14.at[s, d - 1], in_x(d))

    def kv_second(s):
        got('rk', s, dkr1.at[s])
        got('rv', s, dvr1.at[s])
        rows = pl.ds(pl.multiple_of(BLK * y, BLK), BLK)
        dk[s, rows, :] = dk[s, rows, :] + sum(dkr1[s, d - 1] for d in OFFS)
        for n in QUAD:
            rows = sub_rows(Z * n + x)
            dv[s, rows, :] = dv[s, rows, :] + sum(dvr1[s, d - 1, n * SUB:(n + 1) * SUB, :] for d in OFFS)
        for d in OFFS:
            send('sk', s, dk5.at[s, y, rem(x + d)], dkr2.at[s, d - 1], in_x(d))
            send('sv', s, dv5.at[s, rem(y + d), x], dvr2.at[s, d - 1], in_y(d))

    def kv_third(s):
        got('sk', s, dkr2.at[s])
        got('sv', s, dvr2.at[s])
        kst[s] = ((dk[s, sub_rows(m_blk), :] + sum(dkr2[s, d - 1] for d in OFFS)) * SCALE).astype(bf16)
        vst[s] = (dv[s, sub_rows(m_blk), :] + sum(dvr2[s, d - 1] for d in OFFS)).astype(bf16)
        a_s, z_s = group_of(s)
        rows = sub_rows(z)

        @pl.when(g_of(s) == i_own)
        def _():
            dk_fin[rows, :] = kst[s]
            dv_fin[rows, :] = vst[s]

        @pl.when(not_mine(s))
        def _():
            to = dev(a_s, z_s, y, x)
            far = (z_s != z).astype(i32)
            send('fk', far, kst.at[s], dk_fin.at[rows], to)
            send('fv', far, vst.at[s], dv_fin.at[rows], to)

    def bwd_step(n):
        i, lo, _ = bwd_part(n)
        a_i = div(i)
        z_i = rem(i)
        to = 0 if n < 4 else 1
        mine = a == to
        if n in (0, 2):
            when(a == n // 2, dq_room)
        when(mine if n < 6 else mine & (z_i < 2), got, 'ld', z_i, ld.at[i])
        bwd_block(n)

        def give():
            send('g', z_i, acc.at[i], or1.at[z_i], partner)
        if n in (0, 6):
            when(mine, pl.semaphore_wait, room, 1)
        if lo == 0:
            when(mine, give)
        for core, firsts, seconds, thirds, joined in (
                (0, {0: 3, 2: 2, 5: 1, 9: 0}, {2: 3, 5: 2}, {7: 3}, {7: rot(0), 8: rot(1), 9: rot(2)}),
                (1, {1: 3, 3: 2, 5: 1, 9: 0}, {3: 3, 7: 2}, {7: 3}, {1: 3, 2: 2, 3: 1, 5: 0})):
            def events():
                if n in firsts:
                    kv_first(firsts[n])
                if n == 0 and core == 0:
                    for k in (2, 3, 1, 0):
                        pair_done(k)
                    joins()
                if n == 2 and core == 0:
                    for k in (2, 3, 1, 0):
                        col_done(k)
                if n in joined:
                    dq_join(joined[n])
                if n in seconds:
                    kv_second(seconds[n])
                if n in thirds:
                    kv_third(thirds[n])
            when(a == core, events)

    for n in range(STEPS):
        bwd_step(n)

    when(a == 0, dq_join, z)
    kv_second(1)
    kv_third(2)
    sent('kx', k5.at[:, OTHERS, 0])
    sent('ky', k5.at[OTHERS])
    outs = [(k_all.at[0], o_hbm), (k_all.at[1], dq_hbm), (dk_fin, dk_hbm), (dv_fin, dv_hbm)]
    outs = [pltpu.make_async_copy(src, dst, s_sem.at[len(KINDS) + Z + n]) for n, (src, dst) in enumerate(outs)]
    got('oz', 0, or2)
    w_z = [jnp.exp2(get(st_col, z, rem(z + Z - h))[0] - ld[i_own, 0:1, :]) for h in QUAD]
    for ct in TILES:
        cs = tile(ct)
        o = acc[i_own, :, cs] * w_z[0][:, cs]
        for h in OFFS:
            o = o + or2[h - 1, :, cs] * w_z[h][:, cs]
        k_all[0, cs, :] = o.T.astype(bf16)
    outs[0].start()
    kv_second(0)
    kv_third(1)
    got('gz', 0, dqr2)
    for ct in TILES:
        cs = tile(ct)
        k_all[1, cs, :] = ((acc[G + z, :, cs] + sum(dqr2[h - 1, :, cs] for h in OFFS)).T * SCALE).astype(bf16)
    outs[1].start()
    kv_third(0)
    def take(n, rows):
        got('fk', n, dk_fin.at[rows])
        got('fv', n, dv_fin.at[rows])
    take(1, pl.ds(0, BLK - SUB))
    when(jnp.logical_not(keep), take, 0, pl.ds(0, SUB))
    outs[2].start()
    outs[3].start()

    def left(n):
        sent('ka', k_loc.at[pl.ds(0, n * SUB)])
        sent('va', v_loc.at[pl.ds(0, n * SUB)])
        sent('fk', kst.at[pl.ds(0, n)])
        sent('fv', vst.at[pl.ds(0, n)])
    when(keep, left, 3)
    when(jnp.logical_not(keep), left, Z)
    for kind, full in (('q', q_all), ('do', do_all)):
        sent(kind, full.at[OTHERS])
        sent(kind + 'h', full.at[0])
        sent(kind + 'f', full.at[OTHERS])
    for kind, ref in (('vy', v5.at[:, OTHERS, 0]), ('vx', v5.at[OTHERS]), ('st', st_par), ('g', or1), ('ld', ld.at[QUADS]), ('oz', or2), ('gz', dqr2),
                      ('sz', st_col.at[:, OTHERS]), ('rk', dkr1), ('rv', dvr1), ('sk', dkr2), ('sv', dvr2)):
        sent(kind, ref)
    for c in outs:
        c.wait()


def solution(mesh):
    blk_spec = P('data', CTX_AXES, None, None)
    v = pltpu.VMEM
    big = (ROWS, HD)
    big_t = (HD, ROWS)
    blk = (BLK, HD)
    sub = (SUB, HD)
    scratch = [
        *[v(blk, bf16)] * 2,
        *[v((G,) + big, bf16)] * 2, *[v((Z,) + big, bf16)] * 2,
        *[v((Z,) + big_t, bf16)] * 2,
        v((G + Z,) + big_t, f32), *[v((Z,) + big, f32)] * 2,
        v((N_PAIR, ROWS, ROWS), f32),
        v((NT, T, T), f32),
        *[v((G, 1, ROWS), f32)] * 2, v((G, 3, ROWS), f32),
        v((Z, 3, ROWS), f32), v((Z, Z, 3, ROWS), f32), v((G, 2, ROWS), f32),
        v((Z,) + big_t, f32), *[v((3,) + big_t, f32)] * 2,
        *[v((Z, 3) + blk, f32)] * 2,
        *[v((Z, 3) + sub, f32)] * 2, *[v((Z,) + sub, bf16)] * 2,
        *[v(blk, bf16)] * 2,
        pltpu.SemaphoreType.DMA((N_SEND,)), pltpu.SemaphoreType.DMA((N_RECV,)), pltpu.SemaphoreType.REGULAR,
    ]
    call = pl.pallas_call(
        body,
        name='attn',
        out_shape=[jax.ShapeDtypeStruct(big, bf16)] * 2 + [jax.ShapeDtypeStruct(blk, bf16)] * 2,
        in_specs=[pl.BlockSpec(memory_space=pl.ANY)] * 4,
        out_specs=[pl.BlockSpec(memory_space=pl.ANY)] * 4,
        scratch_shapes=scratch,
        compiler_params=pltpu.CompilerParams(collective_id=0, has_side_effects=True, vmem_limit_bytes=67043328),
    )

    def hand_out(*refs):
        srcs, dsts, bufs, sems = refs[:Z], refs[Z:2 * Z], refs[2 * Z:3 * Z], refs[3 * Z]
        ins = [pltpu.make_async_copy(src, buf, sems.at[0, n]) for n, (src, buf) in enumerate(zip(srcs, bufs))]
        outs = [pltpu.make_async_copy(buf, dst, sems.at[1, n]) for n, (buf, dst) in enumerate(zip(bufs, dsts))]
        for c in ins:
            c.start()
        for c, e in zip(ins, outs):
            c.wait()
            e.start()
        for e in outs:
            e.wait()

    leave = pl.pallas_call(
        hand_out,
        name='leave',
        out_shape=[jax.ShapeDtypeStruct(big, bf16)] * 2 + [jax.ShapeDtypeStruct(blk, bf16)] * 2,
        in_specs=[pl.BlockSpec(memory_space=pl.ANY)] * 4,
        out_specs=[pl.BlockSpec(memory_space=pl.ANY)] * 4,
        scratch_shapes=[*[v(big, bf16)] * 2, *[v(blk, bf16)] * 2, pltpu.SemaphoreType.DMA((2, Z))],
    )

    def local_attn(q_in, k_in, v_in, do_in):
        o, dq, dk, dv = leave(*call(q_in.reshape(big), k_in.reshape(blk), v_in.reshape(blk), do_in.reshape(big)))
        return o.reshape(q_in.shape), dq.reshape(q_in.shape), dk.reshape(k_in.shape), dv.reshape(k_in.shape)

    return jax.shard_map(local_attn, mesh=mesh, in_specs=(blk_spec,) * 4, out_specs=(blk_spec,) * 4, check_vma=False)
```

time: 95.1 us -> 89.1 us (0.937)
  Pallas kernels: 94.3 us -> 88.2 us
    pallas_call x1, Pallas kernels: 92.5 us -> 86.4 us  [local_attn(): call(q_in.reshape(big), k_in.reshape(blk), v_in.reshape(blk), do_in.resha...]
where the time goes in v4:
time: 89.1 us; the launch traced here: 89 us
  Pallas kernels  88.2 us (99%)
    pallas_call x1, Pallas kernels, local_attn(): call(q_in.reshape(big), k_in.reshape(blk), v_in.reshape(blk), do_in.resha...  86.4 us
    pallas_call x1, Pallas kernels, local_attn(): leave(*call(q_in.reshape(big), k_in.reshape(blk), v_in.reshape(blk), do_i...  1.79 us

profile of v4, /device:TPU:0, one launch (start us, length us, event | category | flops | bytes accessed | tf_op | source)
XLA Modules:
  0.0 89.0 jit_solution(2539041870022850565)
XLA Ops:
  0.6 86.4 %attn.1 = (bf16[768,128]{1,0:T(8,128)(2,1)}, bf16[768,128]{1,0:T(8,128)(2,1)}, bf16[192,128]{1,0:T(8,128)(2,1)}, bf16[192,128]{1,0:T(8,128)(2,1)}) custom-call(bf16[768,128]{1,0:T(8,128)(2,1)} %bitcast.8, bf16[192,128]{1,0:T(8,128)(2,1)} %bitcast.10, bf16[192,128]{1,0:T(8,128)(2,1)} %bitcast.11, bf16[768,128]{1,0:T(8,128)(2,1)} %bitcast.9), custom_call_target="tpu_custom_call" | custom-call | tf_op jit(solution)/shard_map/attn/pallas_call | solution.py:715
  87.0 1.8 %leave.1 = (bf16[768,128]{1,0:T(8,128)(2,1)}, bf16[768,128]{1,0:T(8,128)(2,1)}, bf16[192,128]{1,0:T(8,128)(2,1)}, bf16[192,128]{1,0:T(8,128)(2,1)}) custom-call(bf16[768,128]{1,0:T(8,128)(2,1)} %get-tuple-element.12.refs_0_, bf16[768,128]{1,0:T(8,128)(2,1)} %get-tuple-element.13.refs_1_, bf16[192,128]{1,0:T(8,128)(2,1)} %get-tuple-element.14.refs_2_, ...), custom_call_target="tpu_custom_call" | custom-call | tf_op jit(solution)/shard_map/leave/pallas_call | solution.py:715

commit v5 on v4

--- a/solution.py
+++ b/solution.py
@@ -394,8 +394,8 @@
 
         @pl.when(a == 1)
         def _():
-            when(e == 0, near_got, 'do', do_all)
-            when(e == 1, far_got, 'do', do_all)
+            when(e == 1, near_got, 'do', do_all)
+            when(e == 2, far_got, 'do', do_all)
 
             @pl.when(e == 1)
             def _():
@@ -434,8 +434,11 @@
             def _():
                 passed_all('do', do_all)
                 lax.fori_loop(Z, G, fwd_done, 0)
+
+            @pl.when(e == 3)
+            def _():
                 out_give()
-                far_got('do', do_all)
+            when(e == 4, far_got, 'do', do_all)
 
             @pl.when(e == 5)
             def _():
@@ -585,8 +588,8 @@
         if lo == 0:
             when(mine, give)
         for core, firsts, seconds, thirds, joined in (
-                (0, {0: 3, 2: 2, 5: 1, 9: 0}, {2: 3, 5: 2}, {7: 3}, {7: rot(0), 8: rot(1), 9: rot(2)}),
-                (1, {1: 3, 3: 2, 5: 1, 9: 0}, {3: 3, 7: 2}, {7: 3}, {1: 3, 2: 2, 3: 1, 5: 0})):
+                (0, {0: 3, 2: 2, 5: 1, 9: 0}, {2: 3, 6: 2}, {}, {7: rot(0), 8: rot(1), 9: rot(2)}),
+                (1, {1: 3, 3: 2, 5: 1, 9: 0}, {3: 3, 8: 2}, {}, {1: 3, 2: 2, 3: 1, 5: 0})):
             def events():
                 if n in firsts:
                     kv_first(firsts[n])
@@ -609,8 +612,6 @@
         bwd_step(n)
 
     when(a == 0, dq_join, z)
-    kv_second(1)
-    kv_third(2)
     sent('kx', k5.at[:, OTHERS, 0])
     sent('ky', k5.at[OTHERS])
     outs = [(k_all.at[0], o_hbm), (k_all.at[1], dq_hbm), (dk_fin, dk_hbm), (dv_fin, dv_hbm)]
@@ -624,6 +625,21 @@
             o = o + or2[h - 1, :, cs] * w_z[h][:, cs]
         k_all[0, cs, :] = o.T.astype(bf16)
     outs[0].start()
+
+    def left(n):
+        sent('ka', k_loc.at[pl.ds(0, n * SUB)])
+        sent('va', v_loc.at[pl.ds(0, n * SUB)])
+    when(keep, left, 3)
+    when(jnp.logical_not(keep), left, Z)
+    for kind, full in (('q', q_all), ('do', do_all)):
+        sent(kind, full.at[OTHERS])
+        sent(kind + 'h', full.at[0])
+        sent(kind + 'f', full.at[OTHERS])
+    for kind, ref in (('vy', v5.at[:, OTHERS, 0]), ('vx', v5.at[OTHERS]), ('st', st_par), ('ld', ld.at[QUADS]), ('oz', or2), ('sz', st_col.at[:, OTHERS])):
+        sent(kind, ref)
+    kv_third(3)
+    kv_second(1)
+    kv_third(2)
     kv_second(0)
     kv_third(1)
     got('gz', 0, dqr2)
@@ -640,20 +656,14 @@
     outs[2].start()
     outs[3].start()
 
-    def left(n):
-        sent('ka', k_loc.at[pl.ds(0, n * SUB)])
-        sent('va', v_loc.at[pl.ds(0, n * SUB)])
+    for kind, ref in (('g', or1), ('gz', dqr2), ('rk', dkr1), ('rv', dvr1), ('sk', dkr2), ('sv', dvr2)):
+        sent(kind, ref)
+
+    def back(n):
         sent('fk', kst.at[pl.ds(0, n)])
         sent('fv', vst.at[pl.ds(0, n)])
-    when(keep, left, 3)
-    when(jnp.logical_not(keep), left, Z)
-    for kind, full in (('q', q_all), ('do', do_all)):
-        sent(kind, full.at[OTHERS])
-        sent(kind + 'h', full.at[0])
-        sent(kind + 'f', full.at[OTHERS])
-    for kind, ref in (('vy', v5.at[:, OTHERS, 0]), ('vx', v5.at[OTHERS]), ('st', st_par), ('g', or1), ('ld', ld.at[QUADS]), ('oz', or2), ('gz', dqr2),
-                      ('sz', st_col.at[:, OTHERS]), ('rk', dkr1), ('rv', dvr1), ('sk', dkr2), ('sv', dvr2)):
-        sent(kind, ref)
+    when(keep, back, 3)
+    when(jnp.logical_not(keep), back, Z)
     for c in outs:
         c.wait()
 

time: 89.1 us -> 87.4 us (0.981)
  Pallas kernels: 88.2 us -> 86.5 us
    pallas_call x1, Pallas kernels: 86.4 us -> 84.7 us  [local_attn(): call(q_in.reshape(big), k_in.reshape(blk), v_in.reshape(blk), do_in.resha...]
where the time goes in v5:
time: 87.4 us; the launch traced here: 87.3 us
  Pallas kernels  86.5 us (99%)
    pallas_call x1, Pallas kernels, local_attn(): call(q_in.reshape(big), k_in.reshape(blk), v_in.reshape(blk), do_in.resha...  84.7 us
    pallas_call x1, Pallas kernels, local_attn(): leave(*call(q_in.reshape(big), k_in.reshape(blk), v_in.reshape(blk), do_i...  1.79 us

profile of v5, /device:TPU:0, one launch (start us, length us, event | category | flops | bytes accessed | tf_op | source)
XLA Modules:
  0.0 87.3 jit_solution(8616320969434200968)
XLA Ops:
  0.6 84.7 %attn.1 = (bf16[768,128]{1,0:T(8,128)(2,1)}, bf16[768,128]{1,0:T(8,128)(2,1)}, bf16[192,128]{1,0:T(8,128)(2,1)}, bf16[192,128]{1,0:T(8,128)(2,1)}) custom-call(bf16[768,128]{1,0:T(8,128)(2,1)} %bitcast.8, bf16[192,128]{1,0:T(8,128)(2,1)} %bitcast.10, bf16[192,128]{1,0:T(8,128)(2,1)} %bitcast.11, bf16[768,128]{1,0:T(8,128)(2,1)} %bitcast.9), custom_call_target="tpu_custom_call" | custom-call | tf_op jit(solution)/shard_map/attn/pallas_call | solution.py:725
  85.3 1.8 %leave.1 = (bf16[768,128]{1,0:T(8,128)(2,1)}, bf16[768,128]{1,0:T(8,128)(2,1)}, bf16[192,128]{1,0:T(8,128)(2,1)}, bf16[192,128]{1,0:T(8,128)(2,1)}) custom-call(bf16[768,128]{1,0:T(8,128)(2,1)} %get-tuple-element.12.refs_0_, bf16[768,128]{1,0:T(8,128)(2,1)} %get-tuple-element.13.refs_1_, bf16[192,128]{1,0:T(8,128)(2,1)} %get-tuple-element.14.refs_2_, ...), custom_call_target="tpu_custom_call" | custom-call | tf_op jit(solution)/shard_map/leave/pallas_call | solution.py:725

commit v6 on v5

--- a/solution.py
+++ b/solution.py
@@ -37,7 +37,7 @@
          'st': Z, 'sz': Z, 'ld': Z, 'o': Z, 'oz': 1, 'g': Z, 'gz': 1,
          'rk': Z, 'rv': Z, 'sk': Z, 'sv': Z, 'fk': 2, 'fv': 2}
 N_RECV = sum(KINDS.values())
-N_SEND = len(KINDS) + 2 * Z
+N_SEND = len(KINDS) + Z
 
 
 def dot(a, b, ca, cb):
@@ -60,7 +60,7 @@
     return pl.ds(pl.multiple_of(SUB * n, SUB), SUB)
 
 
-def body(q_hbm, k_hbm, v_hbm, do_hbm, o_hbm, dq_hbm, dk_hbm, dv_hbm,
+def body(q_hbm, k_hbm, v_hbm, do_hbm, o_out, dq_out, dk_out, dv_out,
          k_loc, v_loc, q_all, do_all, k_all, v_all, kt, vt, acc, dk, dv, cache, dpb,
          m_run, l_run, st_loc, st_par, st_col, ld,
          or1, or2, dqr2, dkr1, dvr1, dkr2, dvr2, kst, vst, dk_fin, dv_fin, s_sem, r_sem, room):
@@ -614,8 +614,6 @@
     when(a == 0, dq_join, z)
     sent('kx', k5.at[:, OTHERS, 0])
     sent('ky', k5.at[OTHERS])
-    outs = [(k_all.at[0], o_hbm), (k_all.at[1], dq_hbm), (dk_fin, dk_hbm), (dv_fin, dv_hbm)]
-    outs = [pltpu.make_async_copy(src, dst, s_sem.at[len(KINDS) + Z + n]) for n, (src, dst) in enumerate(outs)]
     got('oz', 0, or2)
     w_z = [jnp.exp2(get(st_col, z, rem(z + Z - h))[0] - ld[i_own, 0:1, :]) for h in QUAD]
     for ct in TILES:
@@ -623,8 +621,7 @@
         o = acc[i_own, :, cs] * w_z[0][:, cs]
         for h in OFFS:
             o = o + or2[h - 1, :, cs] * w_z[h][:, cs]
-        k_all[0, cs, :] = o.T.astype(bf16)
-    outs[0].start()
+        o_out[cs, :] = o.T.astype(bf16)
 
     def left(n):
         sent('ka', k_loc.at[pl.ds(0, n * SUB)])
@@ -645,16 +642,15 @@
     got('gz', 0, dqr2)
     for ct in TILES:
         cs = tile(ct)
-        k_all[1, cs, :] = ((acc[G + z, :, cs] + sum(dqr2[h - 1, :, cs] for h in OFFS)).T * SCALE).astype(bf16)
-    outs[1].start()
+        dq_out[cs, :] = ((acc[G + z, :, cs] + sum(dqr2[h - 1, :, cs] for h in OFFS)).T * SCALE).astype(bf16)
     kv_third(0)
     def take(n, rows):
         got('fk', n, dk_fin.at[rows])
         got('fv', n, dv_fin.at[rows])
     take(1, pl.ds(0, BLK - SUB))
     when(jnp.logical_not(keep), take, 0, pl.ds(0, SUB))
-    outs[2].start()
-    outs[3].start()
+    dk_out[...] = dk_fin[...]
+    dv_out[...] = dv_fin[...]
 
     for kind, ref in (('g', or1), ('gz', dqr2), ('rk', dkr1), ('rv', dvr1), ('sk', dkr2), ('sv', dvr2)):
         sent(kind, ref)
@@ -664,8 +660,6 @@
         sent('fv', vst.at[pl.ds(0, n)])
     when(keep, back, 3)
     when(jnp.logical_not(keep), back, Z)
-    for c in outs:
-        c.wait()
 
 
 def solution(mesh):
@@ -693,36 +687,32 @@
     call = pl.pallas_call(
         body,
         name='attn',
-        out_shape=[jax.ShapeDtypeStruct(big, bf16)] * 2 + [jax.ShapeDtypeStruct(blk, bf16)] * 2,
+        out_shape=[v(big, bf16), v(big, bf16), v(blk, bf16), v(blk, bf16)],
         in_specs=[pl.BlockSpec(memory_space=pl.ANY)] * 4,
-        out_specs=[pl.BlockSpec(memory_space=pl.ANY)] * 4,
+        out_specs=[pl.BlockSpec(memory_space=pltpu.VMEM)] * 4,
         scratch_shapes=scratch,
-        compiler_params=pltpu.CompilerParams(collective_id=0, has_side_effects=True, vmem_limit_bytes=67043328),
+        compiler_params=pltpu.CompilerParams(collective_id=0, has_side_effects=True, vmem_limit_bytes=66519040),
     )
 
     def hand_out(*refs):
-        srcs, dsts, bufs, sems = refs[:Z], refs[Z:2 * Z], refs[2 * Z:3 * Z], refs[3 * Z]
-        ins = [pltpu.make_async_copy(src, buf, sems.at[0, n]) for n, (src, buf) in enumerate(zip(srcs, bufs))]
-        outs = [pltpu.make_async_copy(buf, dst, sems.at[1, n]) for n, (buf, dst) in enumerate(zip(bufs, dsts))]
-        for c in ins:
+        outs = [pltpu.make_async_copy(src, dst, refs[-1].at[n]) for n, (src, dst) in enumerate(zip(refs[:Z], refs[Z:2 * Z]))]
+        for c in outs:
             c.start()
-        for c, e in zip(ins, outs):
+        for c in outs:
             c.wait()
-            e.start()
-        for e in outs:
-            e.wait()
 
     leave = pl.pallas_call(
         hand_out,
         name='leave',
         out_shape=[jax.ShapeDtypeStruct(big, bf16)] * 2 + [jax.ShapeDtypeStruct(blk, bf16)] * 2,
-        in_specs=[pl.BlockSpec(memory_space=pl.ANY)] * 4,
+        in_specs=[pl.BlockSpec(memory_space=pltpu.VMEM)] * 4,
         out_specs=[pl.BlockSpec(memory_space=pl.ANY)] * 4,
-        scratch_shapes=[*[v(big, bf16)] * 2, *[v(blk, bf16)] * 2, pltpu.SemaphoreType.DMA((2, Z))],
+        scratch_shapes=[pltpu.SemaphoreType.DMA((Z,))],
     )
 
     def local_attn(q_in, k_in, v_in, do_in):
-        o, dq, dk, dv = leave(*call(q_in.reshape(big), k_in.reshape(blk), v_in.reshape(blk), do_in.reshape(big)))
+        kept = call(q_in.reshape(big), k_in.reshape(blk), v_in.reshape(blk), do_in.reshape(big))
+        o, dq, dk, dv = leave(*[pltpu.with_memory_space_constraint(t, pltpu.VMEM) for t in kept])
         return o.reshape(q_in.shape), dq.reshape(q_in.shape), dk.reshape(k_in.shape), dv.reshape(k_in.shape)
 
     return jax.shard_map(local_attn, mesh=mesh, in_specs=(blk_spec,) * 4, out_specs=(blk_spec,) * 4, check_vma=False)

time: 87.4 us -> 86 us (0.984)
  Pallas kernels: 86.5 us -> 84.8 us
    pallas_call x1, Pallas kernels: 1.79 us -> 0.8 us  [local_attn(): leave(*[pltpu.with_memory_space_constraint(t, pltpu.VMEM) for t in kept])]
where the time goes in v6:
time: 86 us; the launch traced here: 85.6 us
  Pallas kernels  84.8 us (99%)
    pallas_call x1, Pallas kernels, local_attn(): call(q_in.reshape(big), k_in.reshape(blk), v_in.reshape(blk), do_in.resha...  84 us

profile of v6, /device:TPU:0, one launch (start us, length us, event | category | flops | bytes accessed | tf_op | source)
XLA Modules:
  0.0 85.6 jit_solution(6699640673104954059)
XLA Ops:
  0.6 84.0 %attn.1 = (bf16[768,128]{1,0:T(8,128)(2,1)S(1)}, bf16[768,128]{1,0:T(8,128)(2,1)S(1)}, bf16[192,128]{1,0:T(8,128)(2,1)S(1)}, bf16[192,128]{1,0:T(8,128)(2,1)S(1)}) custom-call(bf16[768,128]{1,0:T(8,128)(2,1)} %bitcast.8, bf16[192,128]{1,0:T(8,128)(2,1)} %bitcast.10, bf16[192,128]{1,0:T(8,128)(2,1)} %bitcast.11, bf16[768,128]{1,0:T(8,128)(2,1)} %bitcast.9), custom_call_target="tpu_custom_call" | custom-call | tf_op jit(solution)/shard_map/attn/pallas_call | solution.py:714
  84.7 0.8 leave.1
